TPU v7x, 256 devices: a whole 4x4x8 slice. The times are simulated.
256 devices in a mesh: row: 32 (over y, z_hi, x), col: 8 (over z_lo, core).
Axes of the slice: x: 4, y: 4, z: 8 (z_hi: 2, z_lo: 4; z = z_hi * 4 + z_lo), core: 2. Of those that a mesh axis runs over, the one named last changes fastest.
Arguments:
- top_tensor: bfloat16 [2304, 2304], P('row', 'col'), may hold values from -3 to 3
- bottom_tensor: bfloat16 [2304, 2304], P(('col', 'row')), may hold values from -3 to 3
- left_proj: bfloat16 [2304, 48], replicated, may hold values from -0.125 to 0.125
- right_proj: bfloat16 [2304, 48], replicated, may hold values from -0.125 to 0.125
Outputs:
- coarse: bfloat16 [2304, 2304], P(('col', 'row'))
All inputs are finite; a program needn't handle non-finite values.
Results may differ from a plain program's by a relative error of at most 0.0065.
Values may be sent and summed in bfloat16 or wider, within the bound.
A program may use at most 128 MiB of HBM per device.

v0:
```python
import jax
import jax.numpy as jnp
from jax import lax
from jax.sharding import PartitionSpec as P


def copy_for_each(x, axis):
    peers = lax.axis_size(axis)
    return lax.all_to_all(jnp.broadcast_to(x[None], (peers, *x.shape)), axis, 0, 0, tiled=True)


def in_order(parts, dim):
    parts = jnp.moveaxis(parts, 0, dim)
    lengths = parts.shape
    return parts.reshape(*lengths[:dim], lengths[dim] * lengths[dim + 1], *lengths[dim + 2 :])


def collect(x, axis, dim):
    parts = copy_for_each(x, axis)
    return in_order(parts, dim)


def cut_along(x, dim, peers):
    before, after = (x.shape[:dim], x.shape[dim + 1 :])
    return jnp.moveaxis(x.reshape(*before, peers, -1, *after), dim, 0)


def sent_and_summed(x, axis, dim):
    peers = lax.axis_size(axis)
    parts = lax.all_to_all(cut_along(x, dim, peers), axis, 0, 0, tiled=True)
    return jnp.sum(parts.astype(jnp.float32), axis=0)


def place_rows(arrived, window, rows_here, bond_dim, row_count):
    slot_ids = jnp.arange(row_count * window, dtype=jnp.int32)
    source_dev = slot_ids // window
    target_upper = source_dev * rows_here // bond_dim + slot_ids % window
    placing = (target_upper[:, None] == jnp.arange(bond_dim, dtype=jnp.int32)[None, :]).astype(
        jnp.float32
    )
    return jnp.einsum("rsb,su->rub", arrived, placing, precision=lax.Precision.HIGHEST)


def local(top_tensor, bottom_tensor, left_proj, right_proj):
    bond_dim = right_proj.shape[1]
    rows_here = top_tensor.shape[0]
    block_len = top_tensor.shape[1] // bond_dim
    lower_rows = collect(bottom_tensor, "row", 0)
    left_table = left_proj.reshape(bond_dim, bond_dim, bond_dim)
    upper_part = top_tensor.reshape(rows_here, block_len, bond_dim)
    weighted = jnp.einsum(
        "rml,lka->ramk", upper_part, left_table, preferred_element_type=jnp.float32
    )
    weighted = weighted.astype(jnp.bfloat16).reshape(rows_here * bond_dim, block_len * bond_dim)
    window = rows_here // bond_dim + 2
    row_count = lax.axis_size("row")
    start_row = lax.axis_index("row") * rows_here
    first_upper = start_row // bond_dim
    offset_rows = start_row - first_upper * bond_dim
    group_size = 8
    groups = bond_dim // group_size
    column_sets = lower_rows.reshape(block_len * bond_dim, groups, group_size * bond_dim).transpose(
        1, 0, 2
    )

    def one_group(columns):
        product_part = jnp.dot(weighted, columns, preferred_element_type=jnp.float32).astype(
            jnp.bfloat16
        )
        product_part = product_part.reshape(rows_here, bond_dim, group_size, bond_dim)
        padded = jnp.zeros((window * bond_dim, bond_dim, group_size, bond_dim), jnp.bfloat16)
        padded = lax.dynamic_update_slice_in_dim(padded, product_part, offset_rows, 0)
        regrid = padded.reshape(window, bond_dim, bond_dim, group_size, bond_dim).transpose(
            0, 2, 3, 1, 4
        )
        regrid = regrid.reshape(window * bond_dim * group_size, bond_dim * bond_dim)
        projected = jnp.dot(regrid, right_proj, preferred_element_type=jnp.float32)
        return projected.reshape(window, bond_dim, group_size, bond_dim)

    stacked = lax.map(one_group, column_sets)
    per_down = stacked.transpose(0, 3, 2, 1, 4).reshape(bond_dim, bond_dim, window, bond_dim)
    summed = sent_and_summed(per_down.astype(jnp.bfloat16), "col", 0)
    summed = summed.reshape(summed.shape[0] * bond_dim, window, bond_dim)
    arrived = lax.all_to_all(summed, "row", split_axis=0, concat_axis=1, tiled=True)
    combined = place_rows(arrived, window, rows_here, bond_dim, row_count)
    out_rows = combined.shape[0]
    return combined.reshape(out_rows, bond_dim * bond_dim).astype(jnp.bfloat16)


def solution(mesh):
    return jax.shard_map(
        local,
        mesh=mesh,
        in_specs=(P("row", "col"), P(("col", "row"), None), P(), P()),
        out_specs=P(("col", "row"), None),
        check_vma=False,
    )
```

profile of v0, /device:TPU:8, one launch (start us, length us, event | category | flops | bytes accessed | tf_op | source)
XLA Modules:
  0.0 558.9 jit_solution(1294678473184264912)
XLA Ops:
  2.4 14.3 %all-to-all-start = ((bf16[32,9,2304]{2,1,0:T(8,128)(2,1)}), bf16[32,9,2304]{2,1,0:T(8,128)(2,1)}, u32[]{:S(2)}, u32[]{:S(2)}) async-start(bf16[32,9,2304]{2,1,0:T(8,128)(2,1)} %broadcast_in_dim.7), calls=%async_computation | async-start | bytes 4718592 | tf_op jit(solution)/shard_map/all_to_all | solution.py:9
  21.8 11.3 %copy.65 = bf16[72,48,6,48]{3,2,1,0:T(8,128)(2,1)} copy(bf16[72,48,6,48]{0,1,2,3:T(8,128)(2,1)S(1)} %convert_bitcast_fusion) | data formatting | bytes 3981312 | tf_op jit(solution)/shard_map/while | solution.py:80
  33.1 9.5 %reshape.78 = bf16[3456,288]{1,0:T(8,128)(2,1)} reshape(bf16[72,48,6,48]{3,2,1,0:T(8,128)(2,1)} %copy.65) | data formatting | bytes 3981312 | tf_op jit(solution)/shard_map/while | solution.py:80
  42.6 13.0 %all-to-all-done = bf16[32,9,2304]{2,1,0:T(8,128)(2,1)} async-done(((bf16[32,9,2304]{2,1,0:T(8,128)(2,1)}), bf16[32,9,2304]{2,1,0:T(8,128)(2,1)}, u32[]{:S(2)}, u32[]{:S(2)}) %all-to-all-start) | async-done | bytes 1327136 | tf_op jit(solution)/shard_map/all_to_all | solution.py:9
  60.2 430.2 %while.12 = (s32[]{:T(128)}, bf16[6,3,48,8,48]{4,2,1,3,0:T(8,128)(2,1)}, bf16[6,288,384]{2,1,0:T(8,128)(2,1)}, bf16[3456,288]{1,0:T(8,128)(2,1)}, s32[]{:T(128)}...) while((s32[]{:T(128)}, bf16[6,3,48,8,48]{4,2,1,3,0:T(8,128)(2,1)}, bf16[6,288,384]{2,1,0:T(8,128)(2,1)}, ...), condition=%wide.region_1.2_spmd, body=%wide.region_0.1_spmd.sunk | while | flops 1020542976 | bytes 62891608 | solution.py:80
  69.8 7.8 %reshape.85 = bf16[72,48,8,48]{3,2,1,0:T(8,128)(2,1)} reshape(bf16[3456,384]{1,0:T(8,128)(2,1)S(1)} %copy.77) | data formatting | bytes 5308416 | tf_op jit(solution)/shard_map/while/body/eval_jaxpr/reshape | solution.py:70
  77.7 8.6 %broadcast.66 = bf16[144,48,8,48]{3,2,1,0:T(8,128)(2,1)} broadcast(bf16[]{:T(256)} %constant.57.clone.1..sunk), dimensions={} | broadcast | bytes 5308418 | tf_op jit(solution)/shard_map/broadcast.61
  93.0 14.1 %copy.78 = bf16[3,48,8,48,48]{4,3,2,1,0:T(8,128)(2,1)} copy(bf16[3,48,8,48,48]{4,2,1,3,0:T(8,128)(2,1)} %bitcast.60) | data formatting | bytes 10616832 | tf_op jit(solution)/shard_map/while/body/eval_jaxpr/transpose | solution.py:73
  107.1 20.0 %reshape.86 = bf16[3,48,8,2304]{3,2,1,0:T(8,128)(2,1)} reshape(bf16[3,48,8,48,48]{4,3,2,1,0:T(8,128)(2,1)} %copy.78) | data formatting | bytes 10616832 | tf_op jit(solution)/shard_map/reshape.52
  141.5 7.8 %reshape.85 = bf16[72,48,8,48]{3,2,1,0:T(8,128)(2,1)} reshape(bf16[3456,384]{1,0:T(8,128)(2,1)S(1)} %copy.77) | data formatting | bytes 5308416 | tf_op jit(solution)/shard_map/while/body/eval_jaxpr/reshape | solution.py:70
  149.3 8.6 %broadcast.66 = bf16[144,48,8,48]{3,2,1,0:T(8,128)(2,1)} broadcast(bf16[]{:T(256)} %constant.57.clone.1..sunk), dimensions={} | broadcast | bytes 5308418 | tf_op jit(solution)/shard_map/broadcast.61
  164.7 14.1 %copy.78 = bf16[3,48,8,48,48]{4,3,2,1,0:T(8,128)(2,1)} copy(bf16[3,48,8,48,48]{4,2,1,3,0:T(8,128)(2,1)} %bitcast.60) | data formatting | bytes 10616832 | tf_op jit(solution)/shard_map/while/body/eval_jaxpr/transpose | solution.py:73
  178.8 20.0 %reshape.86 = bf16[3,48,8,2304]{3,2,1,0:T(8,128)(2,1)} reshape(bf16[3,48,8,48,48]{4,3,2,1,0:T(8,128)(2,1)} %copy.78) | data formatting | bytes 10616832 | tf_op jit(solution)/shard_map/reshape.52
  213.2 7.8 %reshape.85 = bf16[72,48,8,48]{3,2,1,0:T(8,128)(2,1)} reshape(bf16[3456,384]{1,0:T(8,128)(2,1)S(1)} %copy.77) | data formatting | bytes 5308416 | tf_op jit(solution)/shard_map/while/body/eval_jaxpr/reshape | solution.py:70
  221.0 8.6 %broadcast.66 = bf16[144,48,8,48]{3,2,1,0:T(8,128)(2,1)} broadcast(bf16[]{:T(256)} %constant.57.clone.1..sunk), dimensions={} | broadcast | bytes 5308418 | tf_op jit(solution)/shard_map/broadcast.61
  236.4 14.1 %copy.78 = bf16[3,48,8,48,48]{4,3,2,1,0:T(8,128)(2,1)} copy(bf16[3,48,8,48,48]{4,2,1,3,0:T(8,128)(2,1)} %bitcast.60) | data formatting | bytes 10616832 | tf_op jit(solution)/shard_map/while/body/eval_jaxpr/transpose | solution.py:73
  250.5 20.0 %reshape.86 = bf16[3,48,8,2304]{3,2,1,0:T(8,128)(2,1)} reshape(bf16[3,48,8,48,48]{4,3,2,1,0:T(8,128)(2,1)} %copy.78) | data formatting | bytes 10616832 | tf_op jit(solution)/shard_map/reshape.52
  284.9 7.8 %reshape.85 = bf16[72,48,8,48]{3,2,1,0:T(8,128)(2,1)} reshape(bf16[3456,384]{1,0:T(8,128)(2,1)S(1)} %copy.77) | data formatting | bytes 5308416 | tf_op jit(solution)/shard_map/while/body/eval_jaxpr/reshape | solution.py:70
  292.7 8.6 %broadcast.66 = bf16[144,48,8,48]{3,2,1,0:T(8,128)(2,1)} broadcast(bf16[]{:T(256)} %constant.57.clone.1..sunk), dimensions={} | broadcast | bytes 5308418 | tf_op jit(solution)/shard_map/broadcast.61
  308.1 14.1 %copy.78 = bf16[3,48,8,48,48]{4,3,2,1,0:T(8,128)(2,1)} copy(bf16[3,48,8,48,48]{4,2,1,3,0:T(8,128)(2,1)} %bitcast.60) | data formatting | bytes 10616832 | tf_op jit(solution)/shard_map/while/body/eval_jaxpr/transpose | solution.py:73
  322.2 20.0 %reshape.86 = bf16[3,48,8,2304]{3,2,1,0:T(8,128)(2,1)} reshape(bf16[3,48,8,48,48]{4,3,2,1,0:T(8,128)(2,1)} %copy.78) | data formatting | bytes 10616832 | tf_op jit(solution)/shard_map/reshape.52
  356.6 7.8 %reshape.85 = bf16[72,48,8,48]{3,2,1,0:T(8,128)(2,1)} reshape(bf16[3456,384]{1,0:T(8,128)(2,1)S(1)} %copy.77) | data formatting | bytes 5308416 | tf_op jit(solution)/shard_map/while/body/eval_jaxpr/reshape | solution.py:70
  364.4 8.6 %broadcast.66 = bf16[144,48,8,48]{3,2,1,0:T(8,128)(2,1)} broadcast(bf16[]{:T(256)} %constant.57.clone.1..sunk), dimensions={} | broadcast | bytes 5308418 | tf_op jit(solution)/shard_map/broadcast.61
  379.8 14.1 %copy.78 = bf16[3,48,8,48,48]{4,3,2,1,0:T(8,128)(2,1)} copy(bf16[3,48,8,48,48]{4,2,1,3,0:T(8,128)(2,1)} %bitcast.60) | data formatting | bytes 10616832 | tf_op jit(solution)/shard_map/while/body/eval_jaxpr/transpose | solution.py:73
  393.9 20.0 %reshape.86 = bf16[3,48,8,2304]{3,2,1,0:T(8,128)(2,1)} reshape(bf16[3,48,8,48,48]{4,3,2,1,0:T(8,128)(2,1)} %copy.78) | data formatting | bytes 10616832 | tf_op jit(solution)/shard_map/reshape.52
  428.3 7.8 %reshape.85 = bf16[72,48,8,48]{3,2,1,0:T(8,128)(2,1)} reshape(bf16[3456,384]{1,0:T(8,128)(2,1)S(1)} %copy.77) | data formatting | bytes 5308416 | tf_op jit(solution)/shard_map/while/body/eval_jaxpr/reshape | solution.py:70
  436.1 8.6 %broadcast.66 = bf16[144,48,8,48]{3,2,1,0:T(8,128)(2,1)} broadcast(bf16[]{:T(256)} %constant.57.clone.1..sunk), dimensions={} | broadcast | bytes 5308418 | tf_op jit(solution)/shard_map/broadcast.61
  451.5 14.1 %copy.78 = bf16[3,48,8,48,48]{4,3,2,1,0:T(8,128)(2,1)} copy(bf16[3,48,8,48,48]{4,2,1,3,0:T(8,128)(2,1)} %bitcast.60) | data formatting | bytes 10616832 | tf_op jit(solution)/shard_map/while/body/eval_jaxpr/transpose | solution.py:73
  465.6 20.0 %reshape.86 = bf16[3,48,8,2304]{3,2,1,0:T(8,128)(2,1)} reshape(bf16[3,48,8,48,48]{4,3,2,1,0:T(8,128)(2,1)} %copy.78) | data formatting | bytes 10616832 | tf_op jit(solution)/shard_map/reshape.52
  493.7 39.1 %all_to_all.28 = bf16[8,2,20736]{2,1,0:T(2,128)(2,1)S(1)} all-to-all(bf16[8,2,20736]{2,1,0:T(2,128)(2,1)S(1)} %reshape.79), channel_id=1, replica_groups=mesh['row'=32,'col'=8] {'col'}, dimensions={0} | all-to-all | bytes 1327104 | tf_op jit(solution)/shard_map/all_to_all | solution.py:30
  536.5 7.4 %all-to-all-start.2 = ((f32[32,1,1296]{2,1,0:T(1,128)}), f32[32,1,1296]{2,1,0:T(1,128)S(1)}, u32[]{:S(2)}, u32[]{:S(2)}) async-start(f32[32,1,1296]{2,1,0:T(1,128)} %reshape.81), calls=%async_computation.2 | async-start | bytes 360448 | tf_op jit(solution)/shard_map/all_to_all | solution.py:84
  544.0 11.6 %all-to-all-done.2 = f32[32,1,1296]{2,1,0:T(1,128)S(1)} async-done(((f32[32,1,1296]{2,1,0:T(1,128)}), f32[32,1,1296]{2,1,0:T(1,128)S(1)}, u32[]{:S(2)}, u32[]{:S(2)}) %all-to-all-start.2) | async-done | bytes 165920 | tf_op jit(solution)/shard_map/all_to_all | solution.py:84
  (57 shorter events, 149.3 us)
Async XLA Ops:
  2.4 14.4 %copy-start.1 = (bf16[2304,48]{0,1:T(8,128)(2,1)S(1)}, bf16[2304,48]{0,1:T(8,128)(2,1)}, u32[]{:S(2)}) copy-start(bf16[2304,48]{0,1:T(8,128)(2,1)} %param.8) | copy-start | bytes 663556
  2.4 16.5 %copy-start.2 = (bf16[72,288]{1,0:T(8,128)(2,1)S(1)}, bf16[72,288]{1,0:T(8,128)(2,1)}, u32[]{:S(2)}) copy-start(bf16[72,288]{1,0:T(8,128)(2,1)} %param.6) | copy-start | bytes 124420
  2.4 53.2 %all-to-all-start = ((bf16[32,9,2304]{2,1,0:T(8,128)(2,1)}), bf16[32,9,2304]{2,1,0:T(8,128)(2,1)}, u32[]{:S(2)}, u32[]{:S(2)}) async-start(bf16[32,9,2304]{2,1,0:T(8,128)(2,1)} %broadcast_in_dim.7), calls=%async_computation | async-start | bytes 4718592 | tf_op jit(solution)/shard_map/all_to_all | solution.py:9
  42.6 17.6 %copy-start = (bf16[2304,48]{0,1:T(8,128)(2,1)S(1)}, bf16[2304,48]{0,1:T(8,128)(2,1)}, u32[]{:S(2)}) copy-start(bf16[2304,48]{0,1:T(8,128)(2,1)} %param.9) | copy-start | bytes 663556
  536.5 19.0 %all-to-all-start.2 = ((f32[32,1,1296]{2,1,0:T(1,128)}), f32[32,1,1296]{2,1,0:T(1,128)S(1)}, u32[]{:S(2)}, u32[]{:S(2)}) async-start(f32[32,1,1296]{2,1,0:T(1,128)} %reshape.81), calls=%async_computation.2 | async-start | bytes 360448 | tf_op jit(solution)/shard_map/all_to_all | solution.py:84
where the time goes:
time: 565 us; the launch traced here: 559 us
  local copies, waits for them, and re-layouts  415 us (73%)
  matrix products  56.7 us (10%)
  blocking collectives  39.1 us (7%)
  waiting for transfers between devices  24.6 us (4%)
  starting transfers between devices  21.8 us (4%)
    another operation x12, local copies, waits for them, and re-layouts  172 us
    transpose x6, local copies, waits for them, and re-layouts, one_group(): padded.reshape(window, bond_dim, bond_dim, group_size, bond_dim)  84.5 us
    reshape x6, local copies, waits for them, and re-layouts, one_group(): product_part.reshape(rows_here, bond_dim, group_size, bond_dim)  46.9 us
    dynamic_update_slice x6, local copies, waits for them, and re-layouts, one_group(): lax.dynamic_update_slice_in_dim(padded, product_part, offset_rows, 0)  40.7 us
    all_to_all x1, blocking collectives, sent_and_summed(): parts = lax.all_to_all(cut_along(x, dim, peers), axis, 0, 0, tiled=True)  39.1 us
    dot_general x6, matrix products, one_group(): jnp.dot(weighted, columns, preferred_element_type=jnp.float32)  30.2 us
    convert_element_type x6, local copies, waits for them, and re-layouts, one_group(): jnp.dot(weighted, columns, preferred_element_type=jnp.float32)  27.4 us
    dot_general x6, matrix products, one_group(): projected = jnp.dot(regrid, right_proj, preferred_element_type=jnp.float32)  24.1 us
  transfers between devices with their start and end apart: 2, of which 2 were waited for; matrix products, arithmetic and copies ran while one was open for 5% of the time, Pallas kernels for 0%

commit v1 on v0

v1 whole, which is shorter than its diff:
```python
import jax
import jax.numpy as jnp
from jax import lax
from jax.experimental import pallas as pl
from jax.experimental.pallas import tpu as pltpu
from jax.sharding import PartitionSpec as P

CHI = 48
LANES = 256
PIECE = 16
GROUPS = 10
STEPS = 12


def spread_columns(x):
    lead = x.shape[:-1]
    x = x.reshape(*lead, 8, 6, CHI)
    none = [(0, 0, 0)] * len(lead)
    zero = jnp.zeros((), x.dtype)
    main = x[..., :5, :].reshape(*lead, 8, 5 * CHI)
    main = lax.pad(main, zero, none + [(0, 0, 0), (0, LANES - 5 * CHI, 0)])
    rest = x[..., 5, :].reshape(*lead, 2, 2, 2 * CHI)
    rest = lax.pad(rest, zero, none + [(0, 0, 0), (0, 0, 0), (0, CHI, 0)])
    rest = rest.reshape(*lead, 2, 6 * CHI)[..., :LANES]
    return jnp.concatenate([main, rest], axis=-2)


def left_placing(rows_here):
    lane = jnp.arange(LANES)
    n = lane // PIECE * rows_here + lane % PIECE
    valid = lane % PIECE < rows_here
    l2 = n % CHI
    return ((jnp.arange(CHI)[:, None] == l2[None, :]) & valid[None, :]).astype(jnp.bfloat16)


def right_placing():
    lane = jnp.arange(LANES)
    return (
        (jnp.arange(CHI)[:, None] == (lane % CHI)[None, :]) & (lane < 5 * CHI)[None, :]
    ).astype(jnp.bfloat16)


def f32dot(a, b):
    return jnp.dot(a, b, preferred_element_type=jnp.float32)


def compute_kernel(t1_ref, t2_ref, pl_ref, pr_ref, f_ref, g_ref, out_ref, plt, prt, wf, yb, acc):
    rows_here = 9
    plt[...] = f32dot(pl_ref[...], f_ref[...]).astype(jnp.bfloat16)
    prt[...] = f32dot(pr_ref[...], g_ref[...]).astype(jnp.bfloat16)
    lane = lax.broadcasted_iota(jnp.int32, (CHI, LANES), 1)
    n = lane // PIECE * rows_here + lane % PIECE
    t1 = t1_ref[...]
    zero = jnp.zeros((CHI, LANES), jnp.bfloat16)

    def weigh(a, _):
        w = plt[pl.ds(pl.multiple_of(a * CHI, CHI), CHI), :]
        block = jnp.concatenate(
            [jnp.where((n >= CHI * m) & (n < CHI * (m + 1)), w, zero) for m in range(3)], axis=0
        )
        r = f32dot(t1, block)
        for q in range(4):
            wf[q, pl.ds(a, 72, stride=CHI), :] = r[q // 2 * 72 : q // 2 * 72 + 72, q % 2 * 128 : q % 2 * 128 + 128]
        return _

    lax.fori_loop(0, CHI, weigh, 0)
    acc[...] = jnp.zeros_like(acc)
    p = lax.rem(lax.axis_index("row"), 2)

    def diag(r):
        w = prt[pl.ds(pl.multiple_of(r * CHI, CHI), CHI), :]
        parts = [
            jnp.where((lane >= CHI * e) & (lane < CHI * (e + 1)), w, zero) for e in range(5)
        ]
        return jnp.concatenate(parts + [zero[:16]], axis=0)

    def step(it, _):
        w = jnp.concatenate(
            [wf[q, pl.ds(pl.multiple_of(it * 288, 288), 288), :] for q in range(4)], axis=1
        ).astype(jnp.bfloat16)
        for g in range(GROUPS):
            yb[g] = f32dot(w, t2_ref[:, g * LANES : (g + 1) * LANES]).astype(jnp.bfloat16)
        first = 2 * it + 24 * p
        for start, size, shift in ((0, 96, 0), (96, 48, 24)):
            r = lax.rem(first + shift, CHI)
            weights = jnp.concatenate([diag(r), diag(r + 1)], axis=0)
            left = jnp.concatenate(
                [
                    yb[:, start : start + size, :].reshape(GROUPS * size, LANES),
                    yb[:, 144 + start : 144 + start + size, :].reshape(GROUPS * size, LANES),
                ],
                axis=1,
            )
            z = f32dot(left, weights).reshape(GROUPS, size, LANES)
            acc[:, start : start + size, :] += z
        return _

    lax.fori_loop(0, STEPS, step, 0)
    mid = acc[:, 96:144, :]
    none = jnp.zeros_like(mid)
    out_ref[:, 0:48, :] = (acc[:, 0:48, :] + jnp.where(p == 0, mid, none)).astype(jnp.bfloat16)
    out_ref[:, 48:96, :] = (acc[:, 48:96, :] + jnp.where(p == 0, none, mid)).astype(jnp.bfloat16)


def compute(t1, t2, plr, pr):
    return pl.pallas_call(
        compute_kernel,
        out_shape=jax.ShapeDtypeStruct((GROUPS, 96, LANES), jnp.bfloat16),
        in_specs=[pl.BlockSpec(memory_space=pltpu.VMEM)] * 6,
        out_specs=pl.BlockSpec(memory_space=pltpu.VMEM),
        scratch_shapes=[
            pltpu.VMEM((CHI * CHI, LANES), jnp.bfloat16),
            pltpu.VMEM((CHI * CHI, LANES), jnp.bfloat16),
            pltpu.VMEM((4, 72 * CHI, 128), jnp.float32),
            pltpu.VMEM((GROUPS, 288, LANES), jnp.bfloat16),
            pltpu.VMEM((GROUPS, 144, LANES), jnp.float32),
        ],
        compiler_params=pltpu.CompilerParams(vmem_limit_bytes=56 * 1024 * 1024),
    )(t1, t2, plr, pr, left_placing(9), right_placing())


def local(top_tensor, bottom_tensor, left_proj, right_proj):
    t1 = top_tensor.reshape(3, 24, 2, 144)
    t1 = jnp.stack([t1[0], t1[2], t1[1]], axis=1)
    t1 = t1.transpose(2, 0, 1, 3).reshape(144, 144)
    plr = left_proj.reshape(CHI, CHI, CHI).transpose(2, 0, 1).reshape(CHI * CHI, CHI)

    t2 = spread_columns(bottom_tensor).reshape(9, GROUPS * LANES)
    t2 = lax.all_gather(t2, "row", axis=0)
    t2 = lax.pad(t2, jnp.zeros((), t2.dtype), [(0, 0, 0), (0, PIECE - 9, 0), (0, 0, 0)])
    t2 = t2.reshape(32 * PIECE, GROUPS * LANES)

    part = compute(t1, t2, plr, right_proj)

    main = part[:8, :, : 5 * CHI].reshape(8, 2, CHI, 5, CHI)
    rest = lax.pad(part[8:], jnp.zeros((), part.dtype), [(0, 0, 0), (0, 0, 0), (0, 32, 0)])
    rest = rest.reshape(2, 96, 2, 144)[..., :96].reshape(2, 96, 2, 2, CHI)
    rest = rest.transpose(0, 2, 3, 1, 4).reshape(8, 2, CHI, 1, CHI)
    per_col = jnp.concatenate([main, rest], axis=3)
    got = lax.all_to_all(per_col, "col", 0, 0, tiled=True)
    summed = jnp.sum(got.astype(jnp.float32), axis=0)
    summed = summed.transpose(2, 1, 0, 3).reshape(288, 96)
    arrived = lax.all_to_all(summed.reshape(32, 9, 96), "row", 0, 0, tiled=True)
    arrived = arrived.reshape(16, 2, 9, 2, CHI)
    out = jnp.stack(
        [arrived[:, 0, :, 0], arrived[:, 0, :, 1] + arrived[:, 1, :, 0], arrived[:, 1, :, 1]], axis=1
    )
    return out.transpose(2, 0, 1, 3).reshape(9, CHI * CHI).astype(jnp.bfloat16)


def solution(mesh):
    return jax.shard_map(
        local,
        mesh=mesh,
        in_specs=(P("row", "col"), P(("col", "row"), None), P(), P()),
        out_specs=P(("col", "row"), None),
        check_vma=False,
    )
```

time: 565 us -> 196 us (0.35)
  local copies, waits for them, and re-layouts: 415 us -> 17.9 us
  waiting for transfers between devices: 24.6 us -> 94.2 us
  matrix products: 56.7 us -> 0 us
  Pallas kernels: 0 us -> 29.9 us
  starting transfers between devices: 21.8 us -> 0.01 us
  between operations: 0.18 us -> 13.7 us
    another operation x13 -> x9, local copies, waits for them, and re-layouts: 175 us -> 1.34 us  [the longest x1 0.67 us: local(): t2 = lax.all_gather(t2, 'row', axis=0)]
    all_gather x0 -> x1, waiting for transfers between devices: none -> 94.1 us  [local(): t2 = lax.all_gather(t2, 'row', axis=0)]
    transpose x6 -> x1, local copies, waits for them, and re-layouts: 84.5 us -> 0.17 us  [local(): summed = summed.transpose(2, 1, 0, 3).reshape(288, 96)]
    dot_general x14 -> x0, matrix products: 56.7 us -> none  [the longest x6 30.2 us: one_group(): jnp.dot(weighted, columns, preferred_element_type=jnp.float32)]
    dynamic_update_slice x12 -> x0, local copies, waits for them, and re-layouts: 45.2 us -> none  [the longest x6 40.7 us: one_group(): lax.dynamic_update_slice_in_dim(padded, product_part, offset_rows, 0)]
    reshape x9 -> x8, local copies, waits for them, and re-layouts: 49.2 us -> 4.42 us  [the longest x1 1.66 us: local(): left_proj.reshape(CHI, CHI, CHI).transpose(2, 0, 1).reshape(CHI * CHI, CHI)]
    pallas_call x0 -> x1, Pallas kernels: none -> 29.9 us  [compute(): pl.pallas_call(compute_kernel, out_shape=jax.ShapeDtypeStruct((GROUPS, 96...]
    convert_element_type x7 -> x2, local copies, waits for them, and re-layouts: 28.2 us -> 0.89 us  [local(): return out.transpose(2, 0, 1, 3).reshape(9, CHI * CHI).astype(jnp.bfloat16)]
  transfers between devices with their start and end apart: 2 -> 1, of which waited for: 2 -> 1; matrix products, arithmetic and copies ran while one was open for 5% -> 3% of each run, Pallas kernels for 0% -> 0%
where the time goes in v1:
time: 196 us; the launch traced here: 195 us
  waiting for transfers between devices  94.2 us (48%)
  blocking collectives  34.3 us (17%)
  Pallas kernels  29.9 us (15%)
  local copies, waits for them, and re-layouts  17.9 us (9%)
  between operations  13.7 us (7%)
  other arithmetic  5.23 us (3%)
    all_gather x1, waiting for transfers between devices, local(): t2 = lax.all_gather(t2, 'row', axis=0)  94.1 us
    pallas_call x1, Pallas kernels, compute(): pl.pallas_call(compute_kernel, out_shape=jax.ShapeDtypeStruct((GROUPS, 96...  29.9 us
    all_to_all x1, blocking collectives, local(): arrived = lax.all_to_all(summed.reshape(32, 9, 96), 'row', 0, 0, tiled=True)  18.3 us
    all_to_all x1, blocking collectives, local(): got = lax.all_to_all(per_col, 'col', 0, 0, tiled=True)  16 us
    unnamed x13, local copies, waits for them, and re-layouts  4.44 us
  transfers between devices with their start and end apart: 1, of which 1 were waited for; matrix products, arithmetic and copies ran while one was open for 3% of the time, Pallas kernels for 0%

profile of v1, /device:TPU:8, one launch (start us, length us, event | category | flops | bytes accessed | tf_op | source)
XLA Modules:
  0.0 195.2 jit_solution(14823594553207033084)
XLA Ops:
  6.5 1.1 reshape.109
  7.7 0.1 slice_reduce_fusion
  8.0 0.1 reshape.110
  8.2 0.7 all_gather_reshape.3
  8.9 0.8 fusion.13
  10.1 0.2 maximum_bitcast_fusion.1
  10.3 0.7 reshape.108.t1_ref
  11.0 1.7 reshape.113
  12.6 1.1 copy.43.pr_ref
  13.7 0.6 fusion.4
  14.4 94.1 %all-gather.2.cloned.1.call-done = bf16[32,9,2560]{2,1,0:T(8,128)(2,1)} async-done(((bf16[1,9,2560]{2,1,0:T(8,128)(2,1)}), bf16[32,9,2560]{2,1,0:T(8,128)(2,1)}) %all-gather.2.cloned.1.call-update) | async-done | bytes 1474576 | tf_op jit(solution)/shard_map/all_gather | solution.py:129
  108.5 3.5 %pad.14 = bf16[32,16,2560]{2,1,0:T(8,128)(2,1)} pad(bf16[32,9,2560]{2,1,0:T(8,128)(2,1)} %all-gather.2.cloned.1.call-done, bf16[]{:T(256)} %constant.42.clone.1), padding=0_0x0_7x0_0 | pad | bytes 4096002 | tf_op jit(solution)/shard_map/pad | solution.py:130
  112.1 29.9 %shard_map.46 = bf16[10,96,256]{2,1,0:T(8,128)(2,1)} custom-call(bf16[144,144]{1,0:T(8,128)(2,1)} %reshape.108.t1_ref, bf16[512,2560]{1,0:T(8,128)(2,1)} %bitcast.38, bf16[2304,48]{1,0:T(8,128)(2,1)} %bitcast.39, bf16[2304,48]{1,0:T(8,128)(2,1)} %copy.43.pr_ref, bf16[48,256]{1,0:T(8,128)(2,1)} %get-tuple-element.10.f_ref, ...), custom_call_target="tpu_custom_call" | custom-call | tf_op jit(solution)/shard_map/pallas_call | solution.py:106
  142.0 1.0 slice.60
  143.0 0.2 copy.44
  143.2 0.4 reshape.115
  143.7 0.2 slice-done
  143.9 0.1 copy.53
  144.2 1.9 fusion.14
  146.1 1.8 reshape.121
  147.8 16.0 %all_to_all.10 = bf16[8,2,13824]{2,1,0:T(2,128)(2,1)S(1)} all-to-all(bf16[8,2,13824]{2,1,0:T(2,128)(2,1)S(1)} %reshape.121), channel_id=1, replica_groups=mesh['row'=32,'col'=8] {'col'}, dimensions={0} | all-to-all | bytes 884736 | tf_op jit(solution)/shard_map/all_to_all | solution.py:140
  163.8 1.2 reshape.122
  165.0 1.3 convert_reduce_fusion
  166.3 0.2 copy.47
  166.4 0.2 reshape_reshape.3
  166.7 0.2 reshape.123
  166.9 18.3 %all_to_all.11 = f32[32,1,864]{2,1,0:T(1,128)S(1)} all-to-all(f32[32,1,864]{2,1,0:T(1,128)S(1)} %reshape.123), channel_id=1, replica_groups=mesh['row'=32,'col'=8] {'row'}, dimensions={0} | all-to-all | bytes 221184 | tf_op jit(solution)/shard_map/all_to_all | solution.py:143
  185.2 0.5 broadcast.128
  185.7 0.9 reduce.2
  186.8 0.2 reshape.119
  187.3 0.1 fusion.12
  187.5 0.8 convert_element_type.20
  (34 shorter events, 1.3 us)
Async XLA Ops:
  6.5 4.4 %copy-start = (bf16[2304,48]{0,1:T(8,128)(2,1)S(1)}, bf16[2304,48]{0,1:T(8,128)(2,1)}, u32[]{:S(2)}) copy-start(bf16[2304,48]{0,1:T(8,128)(2,1)} %param.6) | copy-start | bytes 663556
  6.5 102.0 %all-gather.2.cloned.1.call-start = ((), (), s32[]{:S(2)}) async-start(), calls=%async_computation.2 | async-start | bytes 2703360 | tf_op jit(solution)/shard_map/all_gather | solution.py:129
  7.8 4.8 %copy-start.1 = (bf16[2304,48]{0,1:T(8,128)(2,1)S(1)}, bf16[2304,48]{0,1:T(8,128)(2,1)}, u32[]{:S(2)}) copy-start(bf16[2304,48]{0,1:T(8,128)(2,1)} %param.7) | copy-start | bytes 663556
  143.0 0.9 slice-start
Sparse Core Ops, SparseCore 0:
  10.7 97.7 all-gather.1

commit v2 on v1

v2 whole, which is shorter than its diff:
```python
import jax
import jax.numpy as jnp
from jax import lax
from jax.experimental import pallas as pl
from jax.experimental.pallas import tpu as pltpu
from jax.sharding import PartitionSpec as P

CHI = 48
LANES = 256
PIECE = 16
ROWS = 9
GROUPS = 5
STEPS = 12
PEERS = 32
SENDS = 128
MESH = pl.DeviceIdType.MESH
BF16 = jnp.bfloat16
SLOTS = (0, 1, 3, 4)


def spread_columns(x):
    x = x.reshape(ROWS, 4, 2, 6, CHI).transpose(2, 1, 0, 3, 4)
    zero = jnp.zeros((), x.dtype)
    none = (0, 0, 0)
    main = x[:, :, :, :5].reshape(2, 4, ROWS, 5 * CHI)
    main = lax.pad(main, zero, [none, none, none, (0, LANES - 5 * CHI, 0)])
    rest = x[:, :, :, 5].transpose(0, 2, 1, 3).reshape(2, ROWS, 2, 2 * CHI)
    rest = lax.pad(rest, zero, [none, none, none, (0, CHI, 0)])
    rest = rest.reshape(2, 1, ROWS, 6 * CHI)[..., :LANES]
    both = jnp.concatenate([main, rest], axis=1).reshape(2, GROUPS * ROWS, LANES)
    return lax.pad(both, zero, [none, (0, 48 - GROUPS * ROWS, 0), none])


def left_placing():
    lane = jnp.arange(LANES)
    n = lane // PIECE * ROWS + lane % PIECE
    valid = lane % PIECE < ROWS
    return ((jnp.arange(CHI)[:, None] == (n % CHI)[None, :]) & valid[None, :]).astype(BF16)


def right_placing():
    lane = jnp.arange(LANES)
    hit = jnp.arange(CHI)[:, None] == (lane % CHI)[None, :]
    return (hit & (lane < 5 * CHI)[None, :]).astype(BF16)


def row_window(g):
    return min(ROWS * g // 16 * 16, 16)


def row_placing():
    out = []
    to = jnp.arange(8 * PIECE)
    source = jnp.arange(8 * 32)
    for g in range(GROUPS):
        wanted = to // PIECE * 32 + ROWS * g - row_window(g) + to % PIECE
        hit = (wanted[:, None] == source[None, :]) & (to % PIECE < ROWS)[:, None]
        out.append(hit.astype(BF16))
    return jnp.stack(out)


def f32dot(a, b):
    return jnp.dot(a, b, preferred_element_type=jnp.float32)


def kernel(
    t1_ref, t2_ref, pl_ref, pr_ref, f_ref, g_ref, s_ref, out_ref,
    plt, prt, wf, yb, acc, t1s, pieces, t2p, part, extra, from_z, extra_z, rows, ready, arrived,
    sent, t1_got, piece_got, z_got, extra_got, row_got,
):
    i = lax.axis_index("row")
    j = lax.axis_index("col")
    x, zh, y = lax.rem(i, 4), lax.rem(i // 4, 2), i // 8
    core, zl = lax.rem(j, 2), j // 2
    other = 1 - core
    twin = 2 * zl + other

    barrier = pltpu.get_barrier_semaphore()
    for k in range(1, PEERS):
        pl.semaphore_signal(
            barrier, inc=1, device_id={"row": lax.rem(i + k, PEERS)}, device_id_type=MESH
        )
    pl.semaphore_signal(barrier, inc=1, device_id={"col": twin}, device_id_type=MESH)
    zpeers = [(lax.rem(zl + k, 4), 2 * lax.rem(zl + k, 4) + core) for k in range(1, 4)]
    for _, col in zpeers:
        pl.semaphore_signal(barrier, inc=1, device_id={"col": col}, device_id_type=MESH)

    plt[...] = f32dot(pl_ref[...], f_ref[...]).astype(BF16)
    prt[...] = f32dot(pr_ref[...], g_ref[...]).astype(BF16)
    acc[...] = jnp.zeros_like(acc)
    t1s[core] = t1_ref[...]
    pieces[i, core] = t2_ref[core]

    pl.semaphore_wait(barrier, PEERS - 1 + 1 + 3)

    copies = []

    def send(src, dst, got, where):
        copy = pltpu.make_async_remote_copy(
            src_ref=src, dst_ref=dst, send_sem=sent.at[len(copies)], recv_sem=got,
            device_id=where, device_id_type=MESH,
        )
        copy.start()
        copies.append(copy)

    def await_copy(ref, got):
        pltpu.make_async_remote_copy(
            src_ref=ref, dst_ref=ref, send_sem=sent.at[0], recv_sem=got,
            device_id={"col": twin}, device_id_type=MESH,
        ).wait_recv()

    def row_of(dz, dy, dx):
        return (lax.rem(y + dy, 4) * 2 + lax.rem(zh + dz, 2)) * 4 + lax.rem(x + dx, 4)

    def place(cr, dz, a, b):
        return row_of(dz, b, a) if cr == 0 else row_of(dz, a, b)

    def block(cr):
        return core if cr == 0 else other

    def pass_on(cr, dz, a, b, to_z=(), to_a=(), to_b=()):
        source, c = place(cr, dz, a, b), block(cr)
        own = cr == 0 and dz == 0 and a == 0 and b == 0
        src = t2_ref.at[core] if own else pieces.at[source, c]
        targets = [place(cr, 1, 0, 0) for _ in to_z]
        targets += [place(cr, 0, t, 0) for t in to_a] + [place(cr, 0, 0, t) for t in to_b]
        for target in targets:
            send(src, pieces.at[source, c], piece_got.at[source, c], {"row": target})

    def await_piece(cr, dz, a, b):
        source, c = place(cr, dz, a, b), block(cr)
        await_copy(pieces.at[source, c], piece_got.at[source, c])

    lane = lax.broadcasted_iota(jnp.int32, (CHI, LANES), 1)
    n = lane // PIECE * ROWS + lane % PIECE
    zero = jnp.zeros((CHI, LANES), BF16)

    def weigh(a, _):
        w = plt[pl.ds(pl.multiple_of(a * CHI, CHI), CHI), :]
        weights = jnp.concatenate(
            [jnp.where((n >= CHI * m) & (n < CHI * (m + 1)), w, zero) for m in range(3)], axis=0
        )
        r = f32dot(t1s[...].reshape(288, 144), weights)
        for t in range(4):
            for h in range(2):
                wf[2 * t + h, pl.ds(a, 72, stride=CHI), :] = r[
                    72 * t : 72 * t + 72, 128 * h : 128 * h + 128
                ]
        return _

    done = [0]

    def weigh_some(count):
        lax.fori_loop(done[0], done[0] + count, weigh, 0)
        done[0] += count

    send(t2_ref.at[other], pieces.at[i, core], piece_got.at[i, core], {"col": twin})
    send(t1_ref, t1s.at[core], t1_got, {"col": twin})
    pass_on(0, 0, 0, 0, to_z=(1,), to_a=(1, 3), to_b=(1, 3))
    await_piece(1, 0, 0, 0)
    pass_on(1, 0, 0, 0, to_z=(1,), to_a=(1, 3), to_b=(1, 3))
    await_copy(t1_ref, t1_got)
    weigh_some(8)

    def first_axis(dz):
        for cr in range(2):
            await_piece(cr, dz, 3, 0)
            pass_on(cr, dz, 3, 0, to_a=(1,) if dz == 0 else (), to_b=(1, 3))
            await_piece(cr, dz, 1, 0)
            pass_on(cr, dz, 1, 0, to_a=(3,) if dz == 1 else (), to_b=(1, 3))
        weigh_some(8)
        for cr in range(2):
            await_piece(cr, dz, 2, 0)
            pass_on(cr, dz, 2, 0, to_b=(1, 3))

    def second_axis(dz, a):
        for cr in range(2):
            await_piece(cr, dz, a, 3)
            if dz == 0:
                pass_on(cr, dz, a, 3, to_b=(1,))
            await_piece(cr, dz, a, 1)
            if dz == 1:
                pass_on(cr, dz, a, 1, to_b=(3,))

    def second_axis_end(dz, a):
        for cr in range(2):
            await_piece(cr, dz, a, 2)

    first_axis(0)
    for cr in range(2):
        await_piece(cr, 1, 0, 0)
        pass_on(cr, 1, 0, 0, to_a=(1, 3), to_b=(1, 3))
    second_axis(0, 0)
    weigh_some(8)
    second_axis(0, 3)
    second_axis(0, 1)
    first_axis(1)
    second_axis(0, 2)
    second_axis(1, 0)
    weigh_some(8)
    for a in (3, 1, 2):
        second_axis(1, a)
    weigh_some(8)
    for a in (0, 3, 1, 2):
        second_axis_end(0, a)
    for a in (0, 3, 1, 2):
        second_axis_end(1, a)

    for c in range(2):
        for k in range(4):
            for g in range(GROUPS):
                w = row_window(g)
                source = pieces[8 * k : 8 * k + 8, c, w : w + 32, :].reshape(256, LANES)
                t2p[512 * c + 128 * k : 512 * c + 128 * k + 128, LANES * g : LANES * g + LANES] = (
                    f32dot(s_ref[g], source).astype(BF16)
                )

    p = lax.rem(i, 2)

    def diag(r):
        w = prt[pl.ds(pl.multiple_of(r * CHI, CHI), CHI), :]
        parts = [
            jnp.where((lane >= CHI * e) & (lane < CHI * (e + 1)), w, zero) for e in range(5)
        ]
        return jnp.concatenate(parts + [zero[:16]], axis=0)

    def step(it, _):
        w = jnp.concatenate(
            [wf[q, pl.ds(pl.multiple_of(it * 288, 288), 288), :] for q in range(8)], axis=1
        ).astype(BF16)
        for g in range(GROUPS):
            yb[g] = f32dot(w, t2p[:, g * LANES : (g + 1) * LANES]).astype(BF16)
        first = 2 * it + 24 * p
        for start, size, shift in ((0, 96, 0), (96, 48, 24)):
            r = lax.rem(first + shift, CHI)
            weights = jnp.concatenate([diag(r), diag(r + 1)], axis=0)
            left = jnp.concatenate(
                [
                    yb[:, start : start + size, :].reshape(GROUPS * size, LANES),
                    yb[:, 144 + start : 144 + start + size, :].reshape(GROUPS * size, LANES),
                ],
                axis=1,
            )
            z = f32dot(left, weights).reshape(GROUPS, size, LANES)
            acc[:, start : start + size, :] += z
        return _

    lax.fori_loop(0, STEPS, step, 0)

    mid = acc[:, 96:144, :]
    none = jnp.zeros_like(mid)
    part[:, 0:48, :] = (acc[:, 0:48, :] + jnp.where(p == 0, mid, none)).astype(BF16)
    part[:, 48:96, :] = (acc[:, 48:96, :] + jnp.where(p == 0, none, mid)).astype(BF16)
    pad = jnp.zeros((CHI, 32), jnp.float32)
    last = part[4].astype(jnp.float32)
    for z in range(4):
        cut = slice(CHI * SLOTS[z], CHI * SLOTS[z] + CHI)
        extra[z] = jnp.concatenate([last[0:48, cut], last[48:96, cut], pad], axis=1).astype(BF16)
    for z, col in zpeers:
        send(part.at[z], from_z.at[zl], z_got.at[zl], {"col": col})
        send(extra.at[z], extra_z.at[zl], extra_got.at[zl], {"col": col})
    summed = part[zl].astype(jnp.float32)
    sixth = extra[zl].astype(jnp.float32)
    for z, _ in zpeers:
        await_copy(from_z.at[z], z_got.at[z])
        await_copy(extra_z.at[z], extra_got.at[z])
        summed += from_z[z].astype(jnp.float32)
        sixth += extra_z[z].astype(jnp.float32)
    for e in range(5):
        cut = slice(CHI * e, CHI * e + CHI)
        rows[CHI * e : CHI * e + CHI] = jnp.concatenate(
            [summed[0:48, cut], summed[48:96, cut], pad], axis=1
        )
    rows[240:288] = sixth
    rows[288:304] = jnp.zeros((16, 128), jnp.float32)
    for k in range(PEERS):
        ready[k] = rows[ROWS * k : ROWS * k + 16].astype(BF16)

    for k in range(1, PEERS):
        target = lax.rem(i + k, PEERS)
        send(ready.at[target], arrived.at[i], row_got.at[i], {"row": target})
    arrived[i] = ready[i]
    for k in range(1, PEERS):
        source = lax.rem(i + k, PEERS)
        await_copy(arrived.at[source], row_got.at[source])
    blocks = []
    for t in range(16):
        even, odd = arrived[2 * t].astype(jnp.float32), arrived[2 * t + 1].astype(jnp.float32)
        blocks += [even[:, 0:48], even[:, 48:96] + odd[:, 0:48], odd[:, 48:96]]
    out_ref[...] = jnp.concatenate(blocks, axis=1)[0:ROWS].astype(BF16)

    for copy in copies:
        copy.wait_send()


def local(top_tensor, bottom_tensor, left_proj, right_proj):
    t1 = top_tensor.reshape(3, 24, 2, 144)
    t1 = jnp.stack([t1[0], t1[2], t1[1]], axis=1)
    t1 = t1.transpose(2, 0, 1, 3).reshape(144, 144)
    plr = left_proj.reshape(CHI, CHI, CHI).transpose(2, 0, 1).reshape(CHI * CHI, CHI)
    t2 = spread_columns(bottom_tensor)
    dma = pltpu.SemaphoreType.DMA
    return pl.pallas_call(
        kernel,
        out_shape=jax.ShapeDtypeStruct((ROWS, CHI * CHI), BF16),
        in_specs=[pl.BlockSpec(memory_space=pltpu.VMEM)] * 7,
        out_specs=pl.BlockSpec(memory_space=pltpu.VMEM),
        scratch_shapes=[
            pltpu.VMEM((CHI * CHI, LANES), BF16),
            pltpu.VMEM((CHI * CHI, LANES), BF16),
            pltpu.VMEM((8, 72 * CHI, 128), jnp.float32),
            pltpu.VMEM((GROUPS, 288, LANES), BF16),
            pltpu.VMEM((GROUPS, 144, LANES), jnp.float32),
            pltpu.VMEM((2, 144, 144), BF16),
            pltpu.VMEM((PEERS, 2, 48, LANES), BF16),
            pltpu.VMEM((1024, GROUPS * LANES), BF16),
            pltpu.VMEM((GROUPS, 96, LANES), BF16),
            pltpu.VMEM((4, CHI, 128), BF16),
            pltpu.VMEM((4, 96, LANES), BF16),
            pltpu.VMEM((4, CHI, 128), BF16),
            pltpu.VMEM((304, 128), jnp.float32),
            pltpu.VMEM((PEERS, 16, 128), BF16),
            pltpu.VMEM((PEERS, 16, 128), BF16),
            dma((SENDS,)),
            dma,
            dma((PEERS, 2)),
            dma((4,)),
            dma((4,)),
            dma((PEERS,)),
        ],
        compiler_params=pltpu.CompilerParams(
            vmem_limit_bytes=60 * 1024 * 1024, collective_id=0, has_side_effects=True
        ),
    )(t1, t2, plr, right_proj, left_placing(), right_placing(), row_placing())


def solution(mesh):
    return jax.shard_map(
        local,
        mesh=mesh,
        in_specs=(P("row", "col"), P(("col", "row"), None), P(), P()),
        out_specs=P(("col", "row"), None),
        check_vma=False,
    )
```

time: 196 us -> 76.7 us (0.39)
  waiting for transfers between devices: 94.2 us -> 0 us
  Pallas kernels: 29.9 us -> 66.8 us
  blocking collectives: 34.3 us -> 0 us
  between operations: 13.7 us -> 0.22 us
  local copies, waits for them, and re-layouts: 17.9 us -> 7.07 us
  other arithmetic: 5.23 us -> 2.3 us
    all_gather x1 -> x0, waiting for transfers between devices: 94.1 us -> none  [local(): t2 = lax.all_gather(t2, 'row', axis=0)]
    pallas_call x1, Pallas kernels: 29.9 us -> 66.8 us  [local(): pl.pallas_call(kernel, out_shape=jax.ShapeDtypeStruct((ROWS, CHI * CHI),...]
    all_to_all x2 -> x0, blocking collectives: 34.3 us -> none  [the longest x1 18.3 us: local(): arrived = lax.all_to_all(summed.reshape(32, 9, 96), 'row', 0, 0, tiled=True)]
    pad x3 -> x2, local copies, waits for them, and re-layouts: 3.58 us -> 0.64 us  [the longest x1 0.63 us: spread_columns(): return lax.pad(both, zero, [none, (0, 48 - GROUPS * ROWS, 0), none])]
    unnamed x13 -> x10, local copies, waits for them, and re-layouts: 4.44 us -> 3.01 us
  transfers between devices with their start and end apart: 1 -> 0, of which waited for: 1 -> 0; matrix products, arithmetic and copies ran while one was open for 3% -> 0% of each run, Pallas kernels for 0% -> 0%
where the time goes in v2:
time: 76.7 us; the launch traced here: 76.4 us
  Pallas kernels  66.8 us (87%)
  local copies, waits for them, and re-layouts  7.07 us (9%)
  other arithmetic  2.3 us (3%)
    pallas_call x1, Pallas kernels, local(): pl.pallas_call(kernel, out_shape=jax.ShapeDtypeStruct((ROWS, CHI * CHI),...  66.8 us
    unnamed x10, local copies, waits for them, and re-layouts  3.01 us
    reshape x1, local copies, waits for them, and re-layouts, local(): left_proj.reshape(CHI, CHI, CHI).transpose(2, 0, 1).reshape(CHI * CHI, CHI)  1.65 us

profile of v2, /device:TPU:8, one launch (start us, length us, event | category | flops | bytes accessed | tf_op | source)
XLA Modules:
  0.0 76.4 jit_solution(896345374083318848)
XLA Ops:
  0.0 0.0 copy-start.3
  0.1 0.6 fusion.13
  0.8 0.1 copy-done.3
  0.8 0.1 stack_squeeze.9
  1.0 0.1 stack_squeeze.11
  1.1 0.1 stack_squeeze.10
  1.2 0.2 maximum_bitcast_fusion
  1.4 0.0 copy-start.2
  1.4 0.7 reshape.386.t1_ref
  2.1 0.2 copy-done.2
  2.3 0.2 reshape.387
  2.5 0.2 reshape.394
  2.8 0.1 reshape.389
  2.9 0.1 reshape.396
  3.0 0.1 fusion.11
  3.1 0.6 pad.11.t2_ref
  3.8 0.1 fusion.2
  3.9 0.1 fusion.4
  4.0 0.1 fusion.6
  4.1 0.1 fusion.8
  4.2 0.1 fusion.10
  4.4 0.0 copy-start
  4.4 0.8 %stack.15.s_ref = bf16[5,128,256]{2,1,0:T(8,128)(2,1)} convert(pred[5,128,256]{2,1,0:T(8,128)(4,1)S(1)} %fusion.10) | non-fusion elementwise | flops 163840 | bytes 491520 | tf_op jit(solution)/shard_map/stack | solution.py:59
  5.2 0.2 copy-done
  5.3 0.0 copy-start.1
  5.3 1.7 %reshape.392 = bf16[48,48,48]{1,0,2:T(8,128)(2,1)} reshape(bf16[2304,48]{0,1:T(8,128)(2,1)S(1)} %copy-done) | data formatting | bytes 442368 | tf_op jit(solution)/shard_map/reshape | solution.py:300
  7.0 0.0 copy-done.1
  7.0 1.1 %copy.19.pr_ref = bf16[2304,48]{1,0:T(8,128)(2,1)} copy(bf16[2304,48]{0,1:T(8,128)(2,1)S(1)} %copy-done.1) | data formatting | bytes 442368 | tf_op args[3]
  8.1 66.8 %shard_map.46 = bf16[9,2304]{1,0:T(8,128)(2,1)} custom-call(bf16[144,144]{1,0:T(8,128)(2,1)} %reshape.386.t1_ref, bf16[2,48,256]{2,1,0:T(8,128)(2,1)} %pad.11.t2_ref, bf16[2304,48]{1,0:T(8,128)(2,1)} %bitcast.17, bf16[2304,48]{1,0:T(8,128)(2,1)} %copy.19.pr_ref, bf16[48,256]{1,0:T(8,128)(2,1)} %get-tuple-element.8.f_ref, ...), custom_call_target="tpu_custom_call" | custom-call | tf_op jit(solution)/shard_map/pallas_call | solution.py:303
  74.9 1.5 %copy.30 = bf16[9,2304]{1,0:T(8,128)(2,1)} copy(bf16[9,2304]{1,0:T(8,128)(2,1)} %shard_map.46) | data formatting | bytes 82944
  (21 shorter events, 0.4 us)
Async XLA Ops:
  0.0 0.8 %copy-start.3 = (bf16[72,288]{1,0:T(8,128)(2,1)S(1)}, bf16[72,288]{1,0:T(8,128)(2,1)}, u32[]{:S(2)}) copy-start(bf16[72,288]{1,0:T(8,128)(2,1)} %param.4) | copy-start | bytes 124420
  1.4 0.9 %copy-start.2 = (bf16[9,2304]{1,0:T(8,128)(2,1)S(1)}, bf16[9,2304]{1,0:T(8,128)(2,1)}, u32[]{:S(2)}) copy-start(bf16[9,2304]{1,0:T(8,128)(2,1)} %param.5) | copy-start | bytes 124420
  4.4 1.0 %copy-start = (bf16[2304,48]{0,1:T(8,128)(2,1)S(1)}, bf16[2304,48]{0,1:T(8,128)(2,1)}, u32[]{:S(2)}) copy-start(bf16[2304,48]{0,1:T(8,128)(2,1)} %param.6) | copy-start | bytes 663556
  5.3 1.7 %copy-start.1 = (bf16[2304,48]{0,1:T(8,128)(2,1)S(1)}, bf16[2304,48]{0,1:T(8,128)(2,1)}, u32[]{:S(2)}) copy-start(bf16[2304,48]{0,1:T(8,128)(2,1)} %param.7) | copy-start | bytes 663556

commit v3 on v2

v3 whole, which is shorter than its diff:
```python
import jax
import jax.numpy as jnp
from jax import lax
from jax.experimental import pallas as pl
from jax.experimental.pallas import tpu as pltpu
from jax.sharding import PartitionSpec as P

CHI = 48
LANES = 256
PIECE = 16
ROWS = 9
GROUPS = 5
STEPS = 12
OUT = pltpu.VMEM((9, 2304), jnp.bfloat16)
PEERS = 32
SENDS = 128
MESH = pl.DeviceIdType.MESH
BF16 = jnp.bfloat16
SLOTS = (0, 1, 3, 4)


def row_window(g):
    return min(ROWS * g // 16 * 16, 16)


def f32dot(a, b):
    return jnp.dot(a, b, preferred_element_type=jnp.float32)


def one_hot(shape, hit):
    row = lax.broadcasted_iota(jnp.int32, shape, 0)
    col = lax.broadcasted_iota(jnp.int32, shape, 1)
    return jnp.where(hit(row, col), 1.0, 0.0).astype(BF16)


def kernel(
    t1_hbm, t2_hbm, pl_hbm, pr_hbm, out_ref,
    t1_ref, t2_ref, pl_ref, pr_ref, t1x, spread, t2s, plt, prt, wf, yb, acc, t1s, pieces, t2p,
    part, extra, from_z, extra_z, rows, ready, arrived,
    loaded, sent, t1_got, piece_got, z_got, extra_got, row_got,
):
    i = lax.axis_index("row")
    j = lax.axis_index("col")
    x, zh, y = lax.rem(i, 4), lax.rem(i // 4, 2), i // 8
    core, zl = lax.rem(j, 2), j // 2
    other = 1 - core
    twin = 2 * zl + other
    zpeers = [(lax.rem(zl + k, 4), 2 * lax.rem(zl + k, 4) + core) for k in range(1, 4)]

    def row_of(dz, dy, dx):
        return (lax.rem(y + dy, 4) * 2 + lax.rem(zh + dz, 2)) * 4 + lax.rem(x + dx, 4)

    loads = []
    for k, (src, dst) in enumerate(
        ((t2_hbm, t2_ref), (t1_hbm, t1_ref), (pl_hbm, pl_ref), (pr_hbm, pr_ref))
    ):
        loads.append(pltpu.make_async_copy(src, dst, loaded.at[k]))
        loads[-1].start()
    barrier = pltpu.get_barrier_semaphore()
    near = [row_of(0, 0, 1), row_of(0, 0, 3), row_of(0, 1, 0), row_of(0, 3, 0), row_of(1, 0, 0)]
    for peer in near:
        pl.semaphore_signal(barrier, inc=1, device_id={"row": peer}, device_id_type=MESH)
    for col in [twin] + [col for _, col in zpeers]:
        pl.semaphore_signal(barrier, inc=1, device_id={"col": col}, device_id_type=MESH)

    spread[...] = jnp.zeros_like(spread)
    loads[0].wait()
    t2 = t2_ref[...].astype(jnp.float32)
    for c in range(2):
        for z in range(4):
            at = 6 * CHI * (2 * z + c)
            spread[c, ROWS * z : ROWS * z + ROWS, 0 : 5 * CHI] = t2[:, at : at + 5 * CHI]
            slot = CHI * SLOTS[z]
            spread[c, 4 * ROWS : 5 * ROWS, slot : slot + CHI] = t2[:, at + 5 * CHI : at + 6 * CHI]
    t2s[...] = spread[...].astype(BF16)
    pieces[i, core] = t2s[core]
    loads[1].wait()

    pl.semaphore_wait(barrier, 5 + 1 + 3)

    copies = []

    def send(src, dst, got, where):
        copy = pltpu.make_async_remote_copy(
            src_ref=src, dst_ref=dst, send_sem=sent.at[len(copies)], recv_sem=got,
            device_id=where, device_id_type=MESH,
        )
        copy.start()
        copies.append(copy)

    def await_copy(ref, got):
        pltpu.make_async_remote_copy(
            src_ref=ref, dst_ref=ref, send_sem=sent.at[0], recv_sem=got,
            device_id={"col": twin}, device_id_type=MESH,
        ).wait_recv()

    def place(cr, dz, a, b):
        return row_of(dz, b, a) if cr == 0 else row_of(dz, a, b)

    def block(cr):
        return core if cr == 0 else other

    def pass_on(cr, dz, a, b, to_z=(), to_a=(), to_b=()):
        source, c = place(cr, dz, a, b), block(cr)
        own = cr == 0 and dz == 0 and a == 0 and b == 0
        src = t2s.at[core] if own else pieces.at[source, c]
        targets = [place(cr, 1, 0, 0) for _ in to_z]
        targets += [place(cr, 0, t, 0) for t in to_a] + [place(cr, 0, 0, t) for t in to_b]
        for target in targets:
            send(src, pieces.at[source, c], piece_got.at[source, c], {"row": target})

    def await_piece(cr, dz, a, b):
        source, c = place(cr, dz, a, b), block(cr)
        await_copy(pieces.at[source, c], piece_got.at[source, c])

    lane = lax.broadcasted_iota(jnp.int32, (CHI, LANES), 1)
    n = lane // PIECE * ROWS + lane % PIECE
    zero = jnp.zeros((CHI, LANES), BF16)
    swap = one_hot((192, 192), lambda r, c: (r // 8 == c % 24) & (r % 8 == c // 24))

    def weigh(ag, _):
        left = t1s[...]
        results = []
        for k in range(8):
            at = pl.multiple_of((8 * ag + k) * CHI, CHI)
            w = jnp.concatenate([plt[h, pl.ds(at, CHI), :] for h in range(2)], axis=1).astype(BF16)
            weights = jnp.concatenate(
                [jnp.where((n >= CHI * m) & (n < CHI * (m + 1)), w, zero) for m in range(3)], axis=0
            )
            results.append(f32dot(left, weights))
        for t in range(4):
            for s in range(3):
                at = 72 * t + 24 * s
                block = jnp.concatenate([r[at : at + 24] for r in results], axis=0).astype(BF16)
                turned = f32dot(swap, block)
                for q in range(24):
                    to = pl.multiple_of((24 * s + q) * CHI + 8 * ag, 8)
                    wf[pl.ds(to, 8), LANES * t : LANES * t + LANES] = turned[8 * q : 8 * q + 8]
        return _

    done = [0]

    def weigh_some(count):
        lax.fori_loop(done[0], done[0] + count, weigh, 0)
        done[0] += count

    send(t2s.at[other], pieces.at[i, core], piece_got.at[i, core], {"col": twin})
    send(t1_ref, t1x, t1_got, {"col": twin})
    pass_on(0, 0, 0, 0, to_z=(1,), to_a=(1, 3), to_b=(1, 3))
    await_piece(1, 0, 0, 0)
    pass_on(1, 0, 0, 0, to_z=(1,), to_a=(1, 3), to_b=(1, 3))

    place_left = one_hot(
        (CHI, LANES),
        lambda r, c: (r == (c // PIECE * ROWS + c % PIECE) % CHI) & (c % PIECE < ROWS),
    )
    place_right = one_hot((CHI, LANES), lambda r, c: (r == c % CHI) & (c < 5 * CHI))
    loads[2].wait()
    left_proj = pl_ref[...].astype(jnp.float32)
    for k in range(CHI):
        z = f32dot(left_proj[:, CHI * k : CHI * k + CHI].astype(BF16), place_left)
        for h in range(2):
            plt[h, pl.ds(k, CHI, stride=CHI), :] = z[:, 128 * h : 128 * h + 128]
    acc[...] = jnp.zeros_like(acc)
    await_copy(t1x, t1_got)
    mine, theirs = t1_ref[...].astype(jnp.float32), t1x[...].astype(jnp.float32)
    lower = jnp.where(core == 0, mine, theirs)
    upper = jnp.where(core == 0, theirs, mine)
    t1s[...] = jnp.concatenate(
        [lower[:, 0:144], lower[:, 144:288], upper[:, 0:144], upper[:, 144:288]], axis=0
    ).astype(BF16)

    def first_axis(dz):
        for cr in range(2):
            await_piece(cr, dz, 3, 0)
            pass_on(cr, dz, 3, 0, to_a=(1,) if dz == 0 else (), to_b=(1, 3))
            await_piece(cr, dz, 1, 0)
            pass_on(cr, dz, 1, 0, to_a=(3,) if dz == 1 else (), to_b=(1, 3))
        weigh_some(1)
        for cr in range(2):
            await_piece(cr, dz, 2, 0)
            pass_on(cr, dz, 2, 0, to_b=(1, 3))

    def second_axis(dz, a):
        for cr in range(2):
            await_piece(cr, dz, a, 3)
            if dz == 0:
                pass_on(cr, dz, a, 3, to_b=(1,))
            await_piece(cr, dz, a, 1)
            if dz == 1:
                pass_on(cr, dz, a, 1, to_b=(3,))

    def second_axis_end(dz, a):
        for cr in range(2):
            await_piece(cr, dz, a, 2)

    first_axis(0)
    for cr in range(2):
        await_piece(cr, 1, 0, 0)
        pass_on(cr, 1, 0, 0, to_a=(1, 3), to_b=(1, 3))
    second_axis(0, 0)
    weigh_some(1)
    second_axis(0, 3)
    second_axis(0, 1)
    first_axis(1)
    second_axis(0, 2)
    second_axis(1, 0)
    weigh_some(1)
    for a in (3, 1, 2):
        second_axis(1, a)
    weigh_some(1)
    for a in (0, 3, 1, 2):
        second_axis_end(0, a)
    for a in (0, 3, 1, 2):
        second_axis_end(1, a)

    weigh_some(1)
    loads[3].wait()
    prt[...] = lax.dot_general(
        pr_ref[...], place_right, (((0,), (0,)), ((), ())), preferred_element_type=jnp.float32
    ).astype(BF16)

    for g in range(GROUPS):
        w = row_window(g)
        pick = one_hot(
            (8 * PIECE, 256),
            lambda r, c: (c == r // PIECE * 32 + ROWS * g - w + r % PIECE) & (r % PIECE < ROWS),
        )
        for c in range(2):
            for k in range(4):
                source = pieces[8 * k : 8 * k + 8, c, w : w + 32, :].reshape(256, LANES)
                t2p[512 * c + 128 * k : 512 * c + 128 * k + 128, LANES * g : LANES * g + LANES] = (
                    f32dot(pick, source).astype(BF16)
                )

    p = lax.rem(i, 2)

    def diag(r):
        w = prt[pl.ds(pl.multiple_of(r * CHI, CHI), CHI), :]
        parts = [
            jnp.where((lane >= CHI * e) & (lane < CHI * (e + 1)), w, zero) for e in range(5)
        ]
        return jnp.concatenate(parts + [zero[:16]], axis=0)

    def step(it, _):
        starts = [pl.multiple_of((24 * s + 2 * it) * CHI, CHI) for s in (0, 2, 1)]
        w = jnp.concatenate([wf[pl.ds(at, 96), :] for at in starts], axis=0).astype(BF16)
        for g in range(GROUPS):
            yb[g] = f32dot(w, t2p[:, g * LANES : (g + 1) * LANES]).astype(BF16)
        first = 2 * it + 24 * p
        for to, parts, shift in ((0, (0, 96), 0), (96, (192,), 24)):
            r = lax.rem(first + shift, CHI)
            size = CHI * len(parts)
            weights = jnp.concatenate([diag(r), diag(r + 1)], axis=0)
            sides = []
            for k in range(2):
                side = [yb[:, at + CHI * k : at + CHI * k + CHI, :] for at in parts]
                sides.append(jnp.concatenate(side, axis=1).reshape(GROUPS * size, LANES))
            left = jnp.concatenate(sides, axis=1)
            z = f32dot(left, weights).reshape(GROUPS, size, LANES)
            acc[:, to : to + size, :] += z
        return _

    lax.fori_loop(0, STEPS, step, 0)

    mid = acc[:, 96:144, :]
    none = jnp.zeros_like(mid)
    part[:, 0:48, :] = (acc[:, 0:48, :] + jnp.where(p == 0, mid, none)).astype(BF16)
    part[:, 48:96, :] = (acc[:, 48:96, :] + jnp.where(p == 0, none, mid)).astype(BF16)
    pad = jnp.zeros((CHI, 32), jnp.float32)
    last = part[4].astype(jnp.float32)
    for z in range(4):
        cut = slice(CHI * SLOTS[z], CHI * SLOTS[z] + CHI)
        extra[z] = jnp.concatenate([last[0:48, cut], last[48:96, cut], pad], axis=1).astype(BF16)
    for z, col in zpeers:
        send(part.at[z], from_z.at[zl], z_got.at[zl], {"col": col})
        send(extra.at[z], extra_z.at[zl], extra_got.at[zl], {"col": col})
    summed = part[zl].astype(jnp.float32)
    sixth = extra[zl].astype(jnp.float32)
    for z, _ in zpeers:
        await_copy(from_z.at[z], z_got.at[z])
        await_copy(extra_z.at[z], extra_got.at[z])
        summed += from_z[z].astype(jnp.float32)
        sixth += extra_z[z].astype(jnp.float32)
    for e in range(5):
        cut = slice(CHI * e, CHI * e + CHI)
        rows[CHI * e : CHI * e + CHI] = jnp.concatenate(
            [summed[0:48, cut], summed[48:96, cut], pad], axis=1
        )
    rows[240:288] = sixth
    rows[288:304] = jnp.zeros((16, 128), jnp.float32)
    for k in range(PEERS):
        ready[k] = rows[ROWS * k : ROWS * k + 16].astype(BF16)

    for k in range(1, PEERS):
        target = lax.rem(i + k, PEERS)
        send(ready.at[target], arrived.at[i], row_got.at[i], {"row": target})
    arrived[i] = ready[i]
    for k in range(1, PEERS):
        source = lax.rem(i + k, PEERS)
        await_copy(arrived.at[source], row_got.at[source])
    blocks = []
    for t in range(16):
        even, odd = arrived[2 * t].astype(jnp.float32), arrived[2 * t + 1].astype(jnp.float32)
        blocks += [even[:, 0:48], even[:, 48:96] + odd[:, 0:48], odd[:, 48:96]]
    out_ref[...] = jnp.concatenate(blocks, axis=1)[0:ROWS].astype(BF16)

    for copy in copies:
        copy.wait_send()


def local(top_tensor, bottom_tensor, left_proj, right_proj):
    dma = pltpu.SemaphoreType.DMA
    return pl.pallas_call(
        kernel,
        out_shape=OUT,
        in_specs=[pl.BlockSpec(memory_space=pl.ANY)] * 4,
        out_specs=pl.BlockSpec(memory_space=pltpu.VMEM),
        scratch_shapes=[
            pltpu.VMEM((72, 288), BF16),
            pltpu.VMEM((ROWS, CHI * CHI), BF16),
            pltpu.VMEM((CHI, CHI * CHI), BF16),
            pltpu.VMEM((CHI, CHI * CHI), BF16),
            pltpu.VMEM((72, 288), BF16),
            pltpu.VMEM((2, 48, LANES), jnp.float32),
            pltpu.VMEM((2, 48, LANES), BF16),
            pltpu.VMEM((2, CHI * CHI, 128), jnp.float32),
            pltpu.VMEM((CHI * CHI, LANES), BF16),
            pltpu.VMEM((72 * CHI, 4 * LANES), jnp.float32),
            pltpu.VMEM((GROUPS, 288, LANES), BF16),
            pltpu.VMEM((GROUPS, 144, LANES), jnp.float32),
            pltpu.VMEM((288, 144), BF16),
            pltpu.VMEM((PEERS, 2, 48, LANES), BF16),
            pltpu.VMEM((1024, GROUPS * LANES), BF16),
            pltpu.VMEM((GROUPS, 96, LANES), BF16),
            pltpu.VMEM((4, CHI, 128), BF16),
            pltpu.VMEM((4, 96, LANES), BF16),
            pltpu.VMEM((4, CHI, 128), BF16),
            pltpu.VMEM((304, 128), jnp.float32),
            pltpu.VMEM((PEERS, 16, 128), BF16),
            pltpu.VMEM((PEERS, 16, 128), BF16),
            dma((4,)),
            dma((SENDS,)),
            dma,
            dma((PEERS, 2)),
            dma((4,)),
            dma((4,)),
            dma((PEERS,)),
        ],
        compiler_params=pltpu.CompilerParams(
            vmem_limit_bytes=60 * 1024 * 1024, collective_id=0, has_side_effects=True
        ),
    )(top_tensor, bottom_tensor, left_proj.T, right_proj.T)


def solution(mesh):
    return jax.shard_map(
        local,
        mesh=mesh,
        in_specs=(P("row", "col"), P(("col", "row"), None), P(), P()),
        out_specs=P(("col", "row"), None),
        check_vma=False,
    )
```

time: 76.7 us -> 65.9 us (0.86)
  local copies, waits for them, and re-layouts: 7.07 us -> 0.64 us
  other arithmetic: 2.3 us -> 0 us
  Pallas kernels: 66.8 us -> 64.9 us
    reshape x8 -> x0, local copies, waits for them, and re-layouts: 2.92 us -> none  [the longest x1 1.65 us: local(): left_proj.reshape(CHI, CHI, CHI).transpose(2, 0, 1).reshape(CHI * CHI, CHI)]
    unnamed x10 -> x1, local copies, waits for them, and re-layouts: 3.01 us -> 0.64 us
    pallas_call x1, Pallas kernels: 66.8 us -> 64.9 us  [local(): pl.pallas_call(kernel, out_shape=OUT, in_specs=[pl.BlockSpec(memory_space...]
    another operation x2 -> x0, other arithmetic: 0.91 us -> none  [row_placing(): return jnp.stack(out)]
where the time goes in v3:
time: 65.9 us; the launch traced here: 65.6 us
  Pallas kernels  64.9 us (98%)
    pallas_call x1, Pallas kernels, local(): pl.pallas_call(kernel, out_shape=OUT, in_specs=[pl.BlockSpec(memory_space...  64.9 us

profile of v3, /device:TPU:8, one launch (start us, length us, event | category | flops | bytes accessed | tf_op | source)
XLA Modules:
  0.0 65.6 jit_solution(10408547426261921248)
XLA Ops:
  0.0 64.9 %shard_map.46 = bf16[9,2304]{1,0:T(8,128)(2,1)S(1)} custom-call(bf16[72,288]{1,0:T(8,128)(2,1)} %t1_hbm.1, bf16[9,2304]{1,0:T(8,128)(2,1)} %t2_hbm.1, bf16[48,2304]{1,0:T(8,128)(2,1)} %bitcast.2, bf16[48,2304]{1,0:T(8,128)(2,1)} %bitcast.3), custom_call_target="tpu_custom_call" | custom-call | tf_op jit(solution)/shard_map/pallas_call | solution.py:314
  64.9 0.6 copy.6

commit v4 on v3

--- a/solution.py
+++ b/solution.py
@@ -10,10 +10,9 @@
 PIECE = 16
 ROWS = 9
 GROUPS = 5
-STEPS = 12
+NB = 4
 OUT = pltpu.VMEM((9, 2304), jnp.bfloat16)
 PEERS = 32
-SENDS = 128
 MESH = pl.DeviceIdType.MESH
 BF16 = jnp.bfloat16
 SLOTS = (0, 1, 3, 4)
@@ -78,21 +77,23 @@
 
     pl.semaphore_wait(barrier, 5 + 1 + 3)
 
-    copies = []
-
-    def send(src, dst, got, where):
-        copy = pltpu.make_async_remote_copy(
-            src_ref=src, dst_ref=dst, send_sem=sent.at[len(copies)], recv_sem=got,
+    counts = [0] * 6
+
+    def remote(src, dst, kind, got, where):
+        return pltpu.make_async_remote_copy(
+            src_ref=src, dst_ref=dst, send_sem=sent.at[kind], recv_sem=got,
             device_id=where, device_id_type=MESH,
         )
-        copy.start()
-        copies.append(copy)
+
+    def send(kind, src, dst, got, where):
+        remote(src, dst, kind, got, where).start()
+        counts[kind] += 1
 
     def await_copy(ref, got):
-        pltpu.make_async_remote_copy(
-            src_ref=ref, dst_ref=ref, send_sem=sent.at[0], recv_sem=got,
-            device_id={"col": twin}, device_id_type=MESH,
-        ).wait_recv()
+        remote(ref, ref, 0, got, {"col": twin}).wait_recv()
+
+    def await_sent(kind, ref):
+        remote(ref, ref, kind, t1_got, {"col": twin}).wait_send()
 
     def place(cr, dz, a, b):
         return row_of(dz, b, a) if cr == 0 else row_of(dz, a, b)
@@ -107,7 +108,7 @@
         targets = [place(cr, 1, 0, 0) for _ in to_z]
         targets += [place(cr, 0, t, 0) for t in to_a] + [place(cr, 0, 0, t) for t in to_b]
         for target in targets:
-            send(src, pieces.at[source, c], piece_got.at[source, c], {"row": target})
+            send(0, src, pieces.at[source, c], piece_got.at[source, c], {"row": target})
 
     def await_piece(cr, dz, a, b):
         source, c = place(cr, dz, a, b), block(cr)
@@ -144,8 +145,8 @@
         lax.fori_loop(done[0], done[0] + count, weigh, 0)
         done[0] += count
 
-    send(t2s.at[other], pieces.at[i, core], piece_got.at[i, core], {"col": twin})
-    send(t1_ref, t1x, t1_got, {"col": twin})
+    send(5, t2s.at[other], pieces.at[i, core], piece_got.at[i, core], {"col": twin})
+    send(1, t1_ref, t1x, t1_got, {"col": twin})
     pass_on(0, 0, 0, 0, to_z=(1,), to_a=(1, 3), to_b=(1, 3))
     await_piece(1, 0, 0, 0)
     pass_on(1, 0, 0, 0, to_z=(1,), to_a=(1, 3), to_b=(1, 3))
@@ -176,7 +177,8 @@
             pass_on(cr, dz, 3, 0, to_a=(1,) if dz == 0 else (), to_b=(1, 3))
             await_piece(cr, dz, 1, 0)
             pass_on(cr, dz, 1, 0, to_a=(3,) if dz == 1 else (), to_b=(1, 3))
-        weigh_some(1)
+
+    def first_axis_end(dz):
         for cr in range(2):
             await_piece(cr, dz, 2, 0)
             pass_on(cr, dz, 2, 0, to_b=(1, 3))
@@ -194,44 +196,53 @@
         for cr in range(2):
             await_piece(cr, dz, a, 2)
 
+    def pack(dz):
+        for g in range(GROUPS):
+            w = row_window(g)
+            pick = one_hot(
+                (4 * PIECE, 128),
+                lambda r, c: (c == r // PIECE * 32 + ROWS * g - w + r % PIECE) & (r % PIECE < ROWS),
+            )
+            for c in range(2):
+                for k in range(4):
+                    at = pl.multiple_of((2 * k + lax.rem(zh + dz, 2)) * 4, 4)
+                    source = pieces[pl.ds(at, 4), c, w : w + 32, :].reshape(128, LANES)
+                    to = pl.multiple_of(512 * c + PIECE * at, 64)
+                    t2p[pl.ds(to, 64), LANES * g : LANES * g + LANES] = f32dot(
+                        pick, source
+                    ).astype(BF16)
+
     first_axis(0)
+    weigh_some(1)
+    first_axis_end(0)
+    weigh_some(1)
+    second_axis(0, 0)
+    weigh_some(1)
+    second_axis(0, 3)
+    second_axis(0, 1)
+    weigh_some(1)
     for cr in range(2):
         await_piece(cr, 1, 0, 0)
         pass_on(cr, 1, 0, 0, to_a=(1, 3), to_b=(1, 3))
-    second_axis(0, 0)
-    weigh_some(1)
-    second_axis(0, 3)
-    second_axis(0, 1)
+    second_axis(0, 2)
+    weigh_some(1)
     first_axis(1)
-    second_axis(0, 2)
-    second_axis(1, 0)
-    weigh_some(1)
-    for a in (3, 1, 2):
-        second_axis(1, a)
-    weigh_some(1)
+    weigh_some(1)
+    first_axis_end(1)
     for a in (0, 3, 1, 2):
         second_axis_end(0, a)
-    for a in (0, 3, 1, 2):
-        second_axis_end(1, a)
-
-    weigh_some(1)
+    second_axis(1, 0)
     loads[3].wait()
     prt[...] = lax.dot_general(
         pr_ref[...], place_right, (((0,), (0,)), ((), ())), preferred_element_type=jnp.float32
     ).astype(BF16)
-
-    for g in range(GROUPS):
-        w = row_window(g)
-        pick = one_hot(
-            (8 * PIECE, 256),
-            lambda r, c: (c == r // PIECE * 32 + ROWS * g - w + r % PIECE) & (r % PIECE < ROWS),
-        )
-        for c in range(2):
-            for k in range(4):
-                source = pieces[8 * k : 8 * k + 8, c, w : w + 32, :].reshape(256, LANES)
-                t2p[512 * c + 128 * k : 512 * c + 128 * k + 128, LANES * g : LANES * g + LANES] = (
-                    f32dot(pick, source).astype(BF16)
-                )
+    for a in (3, 1):
+        second_axis(1, a)
+    pack(0)
+    second_axis(1, 2)
+    for a in (0, 3, 1, 2):
+        second_axis_end(1, a)
+    pack(1)
 
     p = lax.rem(i, 2)
 
@@ -243,25 +254,25 @@
         return jnp.concatenate(parts + [zero[:16]], axis=0)
 
     def step(it, _):
-        starts = [pl.multiple_of((24 * s + 2 * it) * CHI, CHI) for s in (0, 2, 1)]
-        w = jnp.concatenate([wf[pl.ds(at, 96), :] for at in starts], axis=0).astype(BF16)
+        size = NB * CHI
+        starts = [pl.multiple_of((24 * s + NB * it) * CHI, CHI) for s in (0, 2, 1)]
+        w = jnp.concatenate([wf[pl.ds(at, size), :] for at in starts], axis=0).astype(BF16)
         for g in range(GROUPS):
             yb[g] = f32dot(w, t2p[:, g * LANES : (g + 1) * LANES]).astype(BF16)
-        first = 2 * it + 24 * p
-        for to, parts, shift in ((0, (0, 96), 0), (96, (192,), 24)):
+        first = NB * it + 24 * p
+        for to, parts, shift in ((0, (0, 1), 0), (96, (2,), 24)):
             r = lax.rem(first + shift, CHI)
-            size = CHI * len(parts)
-            weights = jnp.concatenate([diag(r), diag(r + 1)], axis=0)
+            rows_here = CHI * len(parts)
+            weights = jnp.concatenate([diag(r + k) for k in range(NB)], axis=0)
             sides = []
-            for k in range(2):
-                side = [yb[:, at + CHI * k : at + CHI * k + CHI, :] for at in parts]
-                sides.append(jnp.concatenate(side, axis=1).reshape(GROUPS * size, LANES))
-            left = jnp.concatenate(sides, axis=1)
-            z = f32dot(left, weights).reshape(GROUPS, size, LANES)
-            acc[:, to : to + size, :] += z
+            for k in range(NB):
+                side = [yb[:, size * s + CHI * k : size * s + CHI * k + CHI, :] for s in parts]
+                sides.append(jnp.concatenate(side, axis=1).reshape(GROUPS * rows_here, LANES))
+            z = f32dot(jnp.concatenate(sides, axis=1), weights)
+            acc[:, to : to + rows_here, :] += z.reshape(GROUPS, rows_here, LANES)
         return _
 
-    lax.fori_loop(0, STEPS, step, 0)
+    lax.fori_loop(0, 24 // NB, step, 0)
 
     mid = acc[:, 96:144, :]
     none = jnp.zeros_like(mid)
@@ -273,13 +284,13 @@
         cut = slice(CHI * SLOTS[z], CHI * SLOTS[z] + CHI)
         extra[z] = jnp.concatenate([last[0:48, cut], last[48:96, cut], pad], axis=1).astype(BF16)
     for z, col in zpeers:
-        send(part.at[z], from_z.at[zl], z_got.at[zl], {"col": col})
-        send(extra.at[z], extra_z.at[zl], extra_got.at[zl], {"col": col})
+        send(2, part.at[z], from_z.at[zl], z_got, {"col": col})
+        send(3, extra.at[z], extra_z.at[zl], extra_got, {"col": col})
     summed = part[zl].astype(jnp.float32)
     sixth = extra[zl].astype(jnp.float32)
+    await_copy(from_z.at[0:3], z_got)
+    await_copy(extra_z.at[0:3], extra_got)
     for z, _ in zpeers:
-        await_copy(from_z.at[z], z_got.at[z])
-        await_copy(extra_z.at[z], extra_got.at[z])
         summed += from_z[z].astype(jnp.float32)
         sixth += extra_z[z].astype(jnp.float32)
     for e in range(5):
@@ -294,19 +305,22 @@
 
     for k in range(1, PEERS):
         target = lax.rem(i + k, PEERS)
-        send(ready.at[target], arrived.at[i], row_got.at[i], {"row": target})
+        send(4, ready.at[target], arrived.at[i], row_got, {"row": target})
     arrived[i] = ready[i]
-    for k in range(1, PEERS):
-        source = lax.rem(i + k, PEERS)
-        await_copy(arrived.at[source], row_got.at[source])
+    await_copy(arrived.at[0 : PEERS - 1], row_got)
     blocks = []
     for t in range(16):
         even, odd = arrived[2 * t].astype(jnp.float32), arrived[2 * t + 1].astype(jnp.float32)
         blocks += [even[:, 0:48], even[:, 48:96] + odd[:, 0:48], odd[:, 48:96]]
     out_ref[...] = jnp.concatenate(blocks, axis=1)[0:ROWS].astype(BF16)
 
-    for copy in copies:
-        copy.wait_send()
+    assert counts == [2 * (counts[0] // 2), 1, 3, 3, PEERS - 1, 1], counts
+    await_sent(0, pieces.at[0 : counts[0] // 2])
+    await_sent(5, t2s.at[0])
+    await_sent(1, t1x)
+    await_sent(2, from_z.at[0:3])
+    await_sent(3, extra_z.at[0:3])
+    await_sent(4, arrived.at[0 : PEERS - 1])
 
 
 def local(top_tensor, bottom_tensor, left_proj, right_proj):
@@ -327,7 +341,7 @@
             pltpu.VMEM((2, CHI * CHI, 128), jnp.float32),
             pltpu.VMEM((CHI * CHI, LANES), BF16),
             pltpu.VMEM((72 * CHI, 4 * LANES), jnp.float32),
-            pltpu.VMEM((GROUPS, 288, LANES), BF16),
+            pltpu.VMEM((GROUPS, 3 * NB * CHI, LANES), BF16),
             pltpu.VMEM((GROUPS, 144, LANES), jnp.float32),
             pltpu.VMEM((288, 144), BF16),
             pltpu.VMEM((PEERS, 2, 48, LANES), BF16),
@@ -340,12 +354,12 @@
             pltpu.VMEM((PEERS, 16, 128), BF16),
             pltpu.VMEM((PEERS, 16, 128), BF16),
             dma((4,)),
-            dma((SENDS,)),
+            dma((6,)),
             dma,
             dma((PEERS, 2)),
-            dma((4,)),
-            dma((4,)),
-            dma((PEERS,)),
+            dma,
+            dma,
+            dma,
         ],
         compiler_params=pltpu.CompilerParams(
             vmem_limit_bytes=60 * 1024 * 1024, collective_id=0, has_side_effects=True

time: 65.9 us -> 63.5 us (0.964)
  Pallas kernels: 64.9 us -> 62.5 us
    pallas_call x1, Pallas kernels: 64.9 us -> 62.5 us  [local(): pl.pallas_call(kernel, out_shape=OUT, in_specs=[pl.BlockSpec(memory_space...]
where the time goes in v4:
time: 63.5 us; the launch traced here: 63.1 us
  Pallas kernels  62.5 us (98%)
  local copies, waits for them, and re-layouts  0.64 us (1%)
    pallas_call x1, Pallas kernels, local(): pl.pallas_call(kernel, out_shape=OUT, in_specs=[pl.BlockSpec(memory_space...  62.5 us

profile of v4, /device:TPU:8, one launch (start us, length us, event | category | flops | bytes accessed | tf_op | source)
XLA Modules:
  0.0 63.1 jit_solution(4332332985826567461)
XLA Ops:
  0.0 62.5 %shard_map.46 = bf16[9,2304]{1,0:T(8,128)(2,1)S(1)} custom-call(bf16[72,288]{1,0:T(8,128)(2,1)} %t1_hbm.1, bf16[9,2304]{1,0:T(8,128)(2,1)} %t2_hbm.1, bf16[48,2304]{1,0:T(8,128)(2,1)} %bitcast.2, bf16[48,2304]{1,0:T(8,128)(2,1)} %bitcast.3), custom_call_target="tpu_custom_call" | custom-call | tf_op jit(solution)/shard_map/pallas_call | solution.py:328
  62.5 0.6 %copy.6 = bf16[9,2304]{1,0:T(8,128)(2,1)} copy(bf16[9,2304]{1,0:T(8,128)(2,1)S(1)} %shard_map.46) | data formatting | bytes 82944

commit v5 on v4

--- a/solution.py
+++ b/solution.py
@@ -7,8 +7,8 @@
 
 CHI = 48
 LANES = 256
-PIECE = 16
 ROWS = 9
+TILE = 4 * CHI
 GROUPS = 5
 NB = 4
 OUT = pltpu.VMEM((9, 2304), jnp.bfloat16)
@@ -34,7 +34,7 @@
 
 def kernel(
     t1_hbm, t2_hbm, pl_hbm, pr_hbm, out_ref,
-    t1_ref, t2_ref, pl_ref, pr_ref, t1x, spread, t2s, plt, prt, wf, yb, acc, t1s, pieces, t2p,
+    t1_ref, t2_ref, pl_ref, pr_ref, t1x, spread, t2s, plt, prt, wf, yb0, yb1, acc, t1s, pieces, t2p,
     part, extra, from_z, extra_z, rows, ready, arrived,
     loaded, sent, t1_got, piece_got, z_got, extra_got, row_got,
 ):
@@ -115,7 +115,6 @@
         await_copy(pieces.at[source, c], piece_got.at[source, c])
 
     lane = lax.broadcasted_iota(jnp.int32, (CHI, LANES), 1)
-    n = lane // PIECE * ROWS + lane % PIECE
     zero = jnp.zeros((CHI, LANES), BF16)
     swap = one_hot((192, 192), lambda r, c: (r // 8 == c % 24) & (r % 8 == c // 24))
 
@@ -126,10 +125,10 @@
             at = pl.multiple_of((8 * ag + k) * CHI, CHI)
             w = jnp.concatenate([plt[h, pl.ds(at, CHI), :] for h in range(2)], axis=1).astype(BF16)
             weights = jnp.concatenate(
-                [jnp.where((n >= CHI * m) & (n < CHI * (m + 1)), w, zero) for m in range(3)], axis=0
+                [jnp.where((lane >= CHI * m) & (lane < CHI * (m + 1)), w, zero) for m in range(4)], axis=0
             )
             results.append(f32dot(left, weights))
-        for t in range(4):
+        for t in range(3):
             for s in range(3):
                 at = 72 * t + 24 * s
                 block = jnp.concatenate([r[at : at + 24] for r in results], axis=0).astype(BF16)
@@ -151,15 +150,11 @@
     await_piece(1, 0, 0, 0)
     pass_on(1, 0, 0, 0, to_z=(1,), to_a=(1, 3), to_b=(1, 3))
 
-    place_left = one_hot(
-        (CHI, LANES),
-        lambda r, c: (r == (c // PIECE * ROWS + c % PIECE) % CHI) & (c % PIECE < ROWS),
-    )
     place_right = one_hot((CHI, LANES), lambda r, c: (r == c % CHI) & (c < 5 * CHI))
     loads[2].wait()
     left_proj = pl_ref[...].astype(jnp.float32)
     for k in range(CHI):
-        z = f32dot(left_proj[:, CHI * k : CHI * k + CHI].astype(BF16), place_left)
+        z = f32dot(left_proj[:, CHI * k : CHI * k + CHI].astype(BF16), place_right)
         for h in range(2):
             plt[h, pl.ds(k, CHI, stride=CHI), :] = z[:, 128 * h : 128 * h + 128]
     acc[...] = jnp.zeros_like(acc)
@@ -167,9 +162,14 @@
     mine, theirs = t1_ref[...].astype(jnp.float32), t1x[...].astype(jnp.float32)
     lower = jnp.where(core == 0, mine, theirs)
     upper = jnp.where(core == 0, theirs, mine)
+    both = jnp.concatenate([lower, upper], axis=1)
     t1s[...] = jnp.concatenate(
-        [lower[:, 0:144], lower[:, 144:288], upper[:, 0:144], upper[:, 144:288]], axis=0
+        [both[:, TILE * t : TILE * t + TILE] for t in range(3)], axis=0
     ).astype(BF16)
+    for t in range(3):
+        t2p[LANES * t + TILE : LANES * t + LANES, :] = jnp.zeros(
+            (LANES - TILE, GROUPS * LANES), BF16
+        )
 
     def first_axis(dz):
         for cr in range(2):
@@ -196,53 +196,45 @@
         for cr in range(2):
             await_piece(cr, dz, a, 2)
 
-    def pack(dz):
-        for g in range(GROUPS):
-            w = row_window(g)
+    def pack(g):
+        w = row_window(g)
+        for v in range(3):
             pick = one_hot(
-                (4 * PIECE, 128),
-                lambda r, c: (c == r // PIECE * 32 + ROWS * g - w + r % PIECE) & (r % PIECE < ROWS),
+                (CHI, 6 * 32),
+                lambda r, c: c == (r + 3 * v) // ROWS * 32 + ROWS * g - w + (r + 3 * v) % ROWS,
             )
-            for c in range(2):
-                for k in range(4):
-                    at = pl.multiple_of((2 * k + lax.rem(zh + dz, 2)) * 4, 4)
-                    source = pieces[pl.ds(at, 4), c, w : w + 32, :].reshape(128, LANES)
-                    to = pl.multiple_of(512 * c + PIECE * at, 64)
-                    t2p[pl.ds(to, 64), LANES * g : LANES * g + LANES] = f32dot(
-                        pick, source
-                    ).astype(BF16)
+            for m in range(v, 12, 3):
+                first = CHI * (m % 6) // ROWS
+                source = pieces[first : first + 6, m // 6, w : w + 32, :].reshape(192, LANES)
+                to = LANES * (m // 4) + CHI * (m % 4)
+                t2p[to : to + CHI, LANES * g : LANES * g + LANES] = f32dot(pick, source).astype(BF16)
 
     first_axis(0)
-    weigh_some(1)
+    weigh_some(2)
     first_axis_end(0)
-    weigh_some(1)
+    weigh_some(2)
     second_axis(0, 0)
-    weigh_some(1)
     second_axis(0, 3)
     second_axis(0, 1)
-    weigh_some(1)
+    weigh_some(2)
     for cr in range(2):
         await_piece(cr, 1, 0, 0)
         pass_on(cr, 1, 0, 0, to_a=(1, 3), to_b=(1, 3))
     second_axis(0, 2)
-    weigh_some(1)
     first_axis(1)
-    weigh_some(1)
     first_axis_end(1)
     for a in (0, 3, 1, 2):
         second_axis_end(0, a)
     second_axis(1, 0)
+    for a in (3, 1):
+        second_axis(1, a)
     loads[3].wait()
     prt[...] = lax.dot_general(
         pr_ref[...], place_right, (((0,), (0,)), ((), ())), preferred_element_type=jnp.float32
     ).astype(BF16)
-    for a in (3, 1):
-        second_axis(1, a)
-    pack(0)
     second_axis(1, 2)
     for a in (0, 3, 1, 2):
         second_axis_end(1, a)
-    pack(1)
 
     p = lax.rem(i, 2)
 
@@ -253,36 +245,51 @@
         ]
         return jnp.concatenate(parts + [zero[:16]], axis=0)
 
-    def step(it, _):
-        size = NB * CHI
+    size = NB * CHI
+
+    def project(it, yb, k):
+        to, parts, shift = ((0, (0, 1), 0), (96, (2,), 24))[k]
+        r = lax.rem(NB * it + 24 * p + shift, CHI)
+        rows_here = CHI * len(parts)
+        weights = jnp.concatenate([diag(r + k) for k in range(NB)], axis=0)
+        sides = []
+        for k in range(NB):
+            side = [yb[:, size * s + CHI * k : size * s + CHI * k + CHI, :] for s in parts]
+            sides.append(jnp.concatenate(side, axis=1).reshape(GROUPS * rows_here, LANES))
+        z = f32dot(jnp.concatenate(sides, axis=1), weights)
+        acc[:, to : to + rows_here, :] += z.reshape(GROUPS, rows_here, LANES)
+
+    def step(it, yb, other_yb):
         starts = [pl.multiple_of((24 * s + NB * it) * CHI, CHI) for s in (0, 2, 1)]
         w = jnp.concatenate([wf[pl.ds(at, size), :] for at in starts], axis=0).astype(BF16)
         for g in range(GROUPS):
+            if other_yb is None:
+                pack(g)
+            elif g == 1 or g == 3:
+                project(it - 1, other_yb, g // 2)
             yb[g] = f32dot(w, t2p[:, g * LANES : (g + 1) * LANES]).astype(BF16)
-        first = NB * it + 24 * p
-        for to, parts, shift in ((0, (0, 1), 0), (96, (2,), 24)):
-            r = lax.rem(first + shift, CHI)
-            rows_here = CHI * len(parts)
-            weights = jnp.concatenate([diag(r + k) for k in range(NB)], axis=0)
-            sides = []
-            for k in range(NB):
-                side = [yb[:, size * s + CHI * k : size * s + CHI * k + CHI, :] for s in parts]
-                sides.append(jnp.concatenate(side, axis=1).reshape(GROUPS * rows_here, LANES))
-            z = f32dot(jnp.concatenate(sides, axis=1), weights)
-            acc[:, to : to + rows_here, :] += z.reshape(GROUPS, rows_here, LANES)
+
+    def two_steps(k, _):
+        step(2 * k + 1, yb1, yb0)
+        step(2 * k + 2, yb0, yb1)
         return _
 
-    lax.fori_loop(0, 24 // NB, step, 0)
+    last = 24 // NB - 1
+    step(0, yb0, None)
+    lax.fori_loop(0, (last - 1) // 2, two_steps, 0)
+    step(last, yb1, yb0)
+    project(last, yb1, 0)
+    project(last, yb1, 1)
 
     mid = acc[:, 96:144, :]
     none = jnp.zeros_like(mid)
     part[:, 0:48, :] = (acc[:, 0:48, :] + jnp.where(p == 0, mid, none)).astype(BF16)
     part[:, 48:96, :] = (acc[:, 48:96, :] + jnp.where(p == 0, none, mid)).astype(BF16)
     pad = jnp.zeros((CHI, 32), jnp.float32)
-    last = part[4].astype(jnp.float32)
+    sixths = part[4].astype(jnp.float32)
     for z in range(4):
         cut = slice(CHI * SLOTS[z], CHI * SLOTS[z] + CHI)
-        extra[z] = jnp.concatenate([last[0:48, cut], last[48:96, cut], pad], axis=1).astype(BF16)
+        extra[z] = jnp.concatenate([sixths[0:48, cut], sixths[48:96, cut], pad], axis=1).astype(BF16)
     for z, col in zpeers:
         send(2, part.at[z], from_z.at[zl], z_got, {"col": col})
         send(3, extra.at[z], extra_z.at[zl], extra_got, {"col": col})
@@ -340,12 +347,13 @@
             pltpu.VMEM((2, 48, LANES), BF16),
             pltpu.VMEM((2, CHI * CHI, 128), jnp.float32),
             pltpu.VMEM((CHI * CHI, LANES), BF16),
-            pltpu.VMEM((72 * CHI, 4 * LANES), jnp.float32),
+            pltpu.VMEM((72 * CHI, 3 * LANES), jnp.float32),
+            pltpu.VMEM((GROUPS, 3 * NB * CHI, LANES), BF16),
             pltpu.VMEM((GROUPS, 3 * NB * CHI, LANES), BF16),
             pltpu.VMEM((GROUPS, 144, LANES), jnp.float32),
-            pltpu.VMEM((288, 144), BF16),
+            pltpu.VMEM((3 * 72, TILE), BF16),
             pltpu.VMEM((PEERS, 2, 48, LANES), BF16),
-            pltpu.VMEM((1024, GROUPS * LANES), BF16),
+            pltpu.VMEM((3 * LANES, GROUPS * LANES), BF16),
             pltpu.VMEM((GROUPS, 96, LANES), BF16),
             pltpu.VMEM((4, CHI, 128), BF16),
             pltpu.VMEM((4, 96, LANES), BF16),

time: 63.5 us -> 58.2 us (0.917)
  Pallas kernels: 62.5 us -> 57.4 us
    pallas_call x1, Pallas kernels: 62.5 us -> 57.4 us  [local(): pl.pallas_call(kernel, out_shape=OUT, in_specs=[pl.BlockSpec(memory_space...]
where the time goes in v5:
time: 58.2 us; the launch traced here: 58.1 us
  Pallas kernels  57.4 us (99%)
  local copies, waits for them, and re-layouts  0.64 us (1%)
    pallas_call x1, Pallas kernels, local(): pl.pallas_call(kernel, out_shape=OUT, in_specs=[pl.BlockSpec(memory_space...  57.4 us

profile of v5, /device:TPU:8, one launch (start us, length us, event | category | flops | bytes accessed | tf_op | source)
XLA Modules:
  0.0 58.1 jit_solution(6783810038446877770)
XLA Ops:
  0.0 57.4 %shard_map.46 = bf16[9,2304]{1,0:T(8,128)(2,1)S(1)} custom-call(bf16[72,288]{1,0:T(8,128)(2,1)} %t1_hbm.1, bf16[9,2304]{1,0:T(8,128)(2,1)} %t2_hbm.1, bf16[48,2304]{1,0:T(8,128)(2,1)} %bitcast.2, bf16[48,2304]{1,0:T(8,128)(2,1)} %bitcast.3), custom_call_target="tpu_custom_call" | custom-call | tf_op jit(solution)/shard_map/pallas_call | solution.py:335
  57.4 0.6 %copy.6 = bf16[9,2304]{1,0:T(8,128)(2,1)} copy(bf16[9,2304]{1,0:T(8,128)(2,1)S(1)} %shard_map.46) | data formatting | bytes 82944

commit v6 on v5

--- a/solution.py
+++ b/solution.py
@@ -13,6 +13,7 @@
 NB = 4
 OUT = pltpu.VMEM((9, 2304), jnp.bfloat16)
 PEERS = 32
+FAR = (3, 1, 2)
 MESH = pl.DeviceIdType.MESH
 BF16 = jnp.bfloat16
 SLOTS = (0, 1, 3, 4)
@@ -56,7 +57,7 @@
         loads.append(pltpu.make_async_copy(src, dst, loaded.at[k]))
         loads[-1].start()
     barrier = pltpu.get_barrier_semaphore()
-    near = [row_of(0, 0, 1), row_of(0, 0, 3), row_of(0, 1, 0), row_of(0, 3, 0), row_of(1, 0, 0)]
+    near = [row_of(0, 0, k) for k in FAR] + [row_of(0, k, 0) for k in FAR] + [row_of(1, 0, 0)]
     for peer in near:
         pl.semaphore_signal(barrier, inc=1, device_id={"row": peer}, device_id_type=MESH)
     for col in [twin] + [col for _, col in zpeers]:
@@ -75,7 +76,7 @@
     pieces[i, core] = t2s[core]
     loads[1].wait()
 
-    pl.semaphore_wait(barrier, 5 + 1 + 3)
+    pl.semaphore_wait(barrier, 7 + 1 + 3)
 
     counts = [0] * 6
 
@@ -146,9 +147,9 @@
 
     send(5, t2s.at[other], pieces.at[i, core], piece_got.at[i, core], {"col": twin})
     send(1, t1_ref, t1x, t1_got, {"col": twin})
-    pass_on(0, 0, 0, 0, to_z=(1,), to_a=(1, 3), to_b=(1, 3))
+    pass_on(0, 0, 0, 0, to_z=(1,), to_a=FAR, to_b=FAR)
     await_piece(1, 0, 0, 0)
-    pass_on(1, 0, 0, 0, to_z=(1,), to_a=(1, 3), to_b=(1, 3))
+    pass_on(1, 0, 0, 0, to_z=(1,), to_a=FAR, to_b=FAR)
 
     place_right = one_hot((CHI, LANES), lambda r, c: (r == c % CHI) & (c < 5 * CHI))
     loads[2].wait()
@@ -171,30 +172,17 @@
             (LANES - TILE, GROUPS * LANES), BF16
         )
 
-    def first_axis(dz):
+    def relay(dz):
         for cr in range(2):
-            await_piece(cr, dz, 3, 0)
-            pass_on(cr, dz, 3, 0, to_a=(1,) if dz == 0 else (), to_b=(1, 3))
-            await_piece(cr, dz, 1, 0)
-            pass_on(cr, dz, 1, 0, to_a=(3,) if dz == 1 else (), to_b=(1, 3))
-
-    def first_axis_end(dz):
+            for a in FAR:
+                await_piece(cr, dz, a, 0)
+                pass_on(cr, dz, a, 0, to_b=FAR)
+
+    def collect(dz):
         for cr in range(2):
-            await_piece(cr, dz, 2, 0)
-            pass_on(cr, dz, 2, 0, to_b=(1, 3))
-
-    def second_axis(dz, a):
-        for cr in range(2):
-            await_piece(cr, dz, a, 3)
-            if dz == 0:
-                pass_on(cr, dz, a, 3, to_b=(1,))
-            await_piece(cr, dz, a, 1)
-            if dz == 1:
-                pass_on(cr, dz, a, 1, to_b=(3,))
-
-    def second_axis_end(dz, a):
-        for cr in range(2):
-            await_piece(cr, dz, a, 2)
+            for a in (0, *FAR):
+                for b in FAR:
+                    await_piece(cr, dz, a, b)
 
     def pack(g):
         w = row_window(g)
@@ -209,32 +197,20 @@
                 to = LANES * (m // 4) + CHI * (m % 4)
                 t2p[to : to + CHI, LANES * g : LANES * g + LANES] = f32dot(pick, source).astype(BF16)
 
-    first_axis(0)
     weigh_some(2)
-    first_axis_end(0)
-    weigh_some(2)
-    second_axis(0, 0)
-    second_axis(0, 3)
-    second_axis(0, 1)
+    relay(0)
     weigh_some(2)
     for cr in range(2):
         await_piece(cr, 1, 0, 0)
-        pass_on(cr, 1, 0, 0, to_a=(1, 3), to_b=(1, 3))
-    second_axis(0, 2)
-    first_axis(1)
-    first_axis_end(1)
-    for a in (0, 3, 1, 2):
-        second_axis_end(0, a)
-    second_axis(1, 0)
-    for a in (3, 1):
-        second_axis(1, a)
+        pass_on(cr, 1, 0, 0, to_a=FAR, to_b=FAR)
+    weigh_some(2)
+    relay(1)
     loads[3].wait()
     prt[...] = lax.dot_general(
         pr_ref[...], place_right, (((0,), (0,)), ((), ())), preferred_element_type=jnp.float32
     ).astype(BF16)
-    second_axis(1, 2)
-    for a in (0, 3, 1, 2):
-        second_axis_end(1, a)
+    collect(0)
+    collect(1)
 
     p = lax.rem(i, 2)
 

time: 58.2 us -> 51.1 us (0.88)
  Pallas kernels: 57.4 us -> 49.9 us
    pallas_call x1, Pallas kernels: 57.4 us -> 49.9 us  [local(): pl.pallas_call(kernel, out_shape=OUT, in_specs=[pl.BlockSpec(memory_space...]
where the time goes in v6:
time: 51.1 us; the launch traced here: 50.5 us
  Pallas kernels  49.9 us (98%)
  local copies, waits for them, and re-layouts  0.64 us (1%)
    pallas_call x1, Pallas kernels, local(): pl.pallas_call(kernel, out_shape=OUT, in_specs=[pl.BlockSpec(memory_space...  49.9 us

profile of v6, /device:TPU:8, one launch (start us, length us, event | category | flops | bytes accessed | tf_op | source)
XLA Modules:
  0.0 50.5 jit_solution(6124719826463153680)
XLA Ops:
  0.0 49.9 %shard_map.46 = bf16[9,2304]{1,0:T(8,128)(2,1)S(1)} custom-call(bf16[72,288]{1,0:T(8,128)(2,1)} %t1_hbm.1, bf16[9,2304]{1,0:T(8,128)(2,1)} %t2_hbm.1, bf16[48,2304]{1,0:T(8,128)(2,1)} %bitcast.2, bf16[48,2304]{1,0:T(8,128)(2,1)} %bitcast.3), custom_call_target="tpu_custom_call" | custom-call | tf_op jit(solution)/shard_map/pallas_call | solution.py:311
  49.9 0.6 %copy.6 = bf16[9,2304]{1,0:T(8,128)(2,1)} copy(bf16[9,2304]{1,0:T(8,128)(2,1)S(1)} %shard_map.46) | data formatting | bytes 82944

commit v7 on v6

--- a/solution.py
+++ b/solution.py
@@ -10,7 +10,8 @@
 ROWS = 9
 TILE = 4 * CHI
 GROUPS = 5
-NB = 4
+SLOTS_HERE = 12
+STEP = SLOTS_HERE * CHI
 OUT = pltpu.VMEM((9, 2304), jnp.bfloat16)
 PEERS = 32
 FAR = (3, 1, 2)
@@ -35,9 +36,9 @@
 
 def kernel(
     t1_hbm, t2_hbm, pl_hbm, pr_hbm, out_ref,
-    t1_ref, t2_ref, pl_ref, pr_ref, t1x, spread, t2s, plt, prt, wf, yb0, yb1, acc, t1s, pieces, t2p,
-    part, extra, from_z, extra_z, rows, ready, arrived,
-    loaded, sent, t1_got, piece_got, z_got, extra_got, row_got,
+    t1_ref, t2_ref, pl_ref, pr_ref, t1x, spread, t2s, plt, prt, wf, yb0, yb1, acc_half, acc_whole, t1s, pieces, t2p,
+    part, from_z, rows, ready, arrived,
+    loaded, sent, t1_got, piece_got, z_got, row_got,
 ):
     i = lax.axis_index("row")
     j = lax.axis_index("col")
@@ -158,7 +159,8 @@
         z = f32dot(left_proj[:, CHI * k : CHI * k + CHI].astype(BF16), place_right)
         for h in range(2):
             plt[h, pl.ds(k, CHI, stride=CHI), :] = z[:, 128 * h : 128 * h + 128]
-    acc[...] = jnp.zeros_like(acc)
+    acc_half[...] = jnp.zeros_like(acc_half)
+    acc_whole[...] = jnp.zeros_like(acc_whole)
     await_copy(t1x, t1_got)
     mine, theirs = t1_ref[...].astype(jnp.float32), t1x[...].astype(jnp.float32)
     lower = jnp.where(core == 0, mine, theirs)
@@ -221,67 +223,75 @@
         ]
         return jnp.concatenate(parts + [zero[:16]], axis=0)
 
-    size = NB * CHI
-
-    def project(it, yb, k):
-        to, parts, shift = ((0, (0, 1), 0), (96, (2,), 24))[k]
-        r = lax.rem(NB * it + 24 * p + shift, CHI)
-        rows_here = CHI * len(parts)
-        weights = jnp.concatenate([diag(r + k) for k in range(NB)], axis=0)
-        sides = []
-        for k in range(NB):
-            side = [yb[:, size * s + CHI * k : size * s + CHI * k + CHI, :] for s in parts]
-            sides.append(jnp.concatenate(side, axis=1).reshape(GROUPS * rows_here, LANES))
-        z = f32dot(jnp.concatenate(sides, axis=1), weights)
-        acc[:, to : to + rows_here, :] += z.reshape(GROUPS, rows_here, LANES)
-
-    def step(it, yb, other_yb):
-        starts = [pl.multiple_of((24 * s + NB * it) * CHI, CHI) for s in (0, 2, 1)]
-        w = jnp.concatenate([wf[pl.ds(at, size), :] for at in starts], axis=0).astype(BF16)
+    base = (48 * (1 - p), 24 * p)
+
+    def project(slot, yb, total):
+        r = lax.rem(24 * p + slot, CHI)
+        for k in range(0, SLOTS_HERE, 4):
+            weights = jnp.concatenate([diag(r + k + q) for q in range(4)], axis=0)
+            left = [
+                yb[:, CHI * (k + q) : CHI * (k + q + 1), :].reshape(GROUPS * CHI, LANES)
+                for q in range(4)
+            ]
+            z = f32dot(jnp.concatenate(left, axis=1), weights)
+            total[...] += z.reshape(GROUPS, CHI, LANES)
+
+    def multiply(slot, yb, before=None):
+        w = wf[pl.ds(pl.multiple_of(slot * CHI, CHI), STEP), :].astype(BF16)
         for g in range(GROUPS):
-            if other_yb is None:
+            if before is None:
                 pack(g)
-            elif g == 1 or g == 3:
-                project(it - 1, other_yb, g // 2)
+            elif g == 1:
+                project(*before)
             yb[g] = f32dot(w, t2p[:, g * LANES : (g + 1) * LANES]).astype(BF16)
 
-    def two_steps(k, _):
-        step(2 * k + 1, yb1, yb0)
-        step(2 * k + 2, yb0, yb1)
-        return _
-
-    last = 24 // NB - 1
-    step(0, yb0, None)
-    lax.fori_loop(0, (last - 1) // 2, two_steps, 0)
-    step(last, yb1, yb0)
-    project(last, yb1, 0)
-    project(last, yb1, 1)
-
-    mid = acc[:, 96:144, :]
-    none = jnp.zeros_like(mid)
-    part[:, 0:48, :] = (acc[:, 0:48, :] + jnp.where(p == 0, mid, none)).astype(BF16)
-    part[:, 48:96, :] = (acc[:, 48:96, :] + jnp.where(p == 0, none, mid)).astype(BF16)
+    gap = jnp.zeros((16, 16), jnp.float32)
+    wide_gap = jnp.zeros((16, 64), jnp.float32)
+
+    def send_part(u, total):
+        for z in range(4):
+            part[u, z, 0:48, :] = total[z].astype(BF16)
+            at = CHI * SLOTS[z]
+            sixth = total[4][:, at : at + CHI]
+            parts = []
+            for q in range(3):
+                parts += [sixth[16 * q : 16 * q + 16], gap]
+            part[u, z, 48:64, :] = jnp.concatenate(parts + [wide_gap], axis=1).astype(BF16)
+        for z, col in zpeers:
+            send(2 + u, part.at[u, z], from_z.at[u, zl], z_got.at[u], {"col": col})
+
+    jobs = [(base[0] + SLOTS_HERE * k, acc_half) for k in range(2)]
+    jobs += [(base[1] + SLOTS_HERE * k, acc_whole) for k in range(4)]
+    before = None
+    for k, (slot, total) in enumerate(jobs):
+        yb = (yb0, yb1)[k % 2]
+        multiply(slot, yb, before)
+        before = (slot, yb, total)
+        if k == 2:
+            send_part(0, acc_half)
+    project(*before)
+    send_part(1, acc_whole)
+
+    summed = []
+    for u in range(2):
+        await_copy(from_z.at[u, 0:3], z_got.at[u])
+        value = part[u, zl].astype(jnp.float32)
+        for z, _ in zpeers:
+            value += from_z[u, z].astype(jnp.float32)
+        summed.append(value)
+    first = jnp.where(p == 0, summed[1], summed[0])
+    second = jnp.where(p == 0, summed[0], summed[1])
     pad = jnp.zeros((CHI, 32), jnp.float32)
-    sixths = part[4].astype(jnp.float32)
-    for z in range(4):
-        cut = slice(CHI * SLOTS[z], CHI * SLOTS[z] + CHI)
-        extra[z] = jnp.concatenate([sixths[0:48, cut], sixths[48:96, cut], pad], axis=1).astype(BF16)
-    for z, col in zpeers:
-        send(2, part.at[z], from_z.at[zl], z_got, {"col": col})
-        send(3, extra.at[z], extra_z.at[zl], extra_got, {"col": col})
-    summed = part[zl].astype(jnp.float32)
-    sixth = extra[zl].astype(jnp.float32)
-    await_copy(from_z.at[0:3], z_got)
-    await_copy(extra_z.at[0:3], extra_got)
-    for z, _ in zpeers:
-        summed += from_z[z].astype(jnp.float32)
-        sixth += extra_z[z].astype(jnp.float32)
     for e in range(5):
         cut = slice(CHI * e, CHI * e + CHI)
         rows[CHI * e : CHI * e + CHI] = jnp.concatenate(
-            [summed[0:48, cut], summed[48:96, cut], pad], axis=1
+            [first[0:48, cut], second[0:48, cut], pad], axis=1
         )
-    rows[240:288] = sixth
+    for q in range(3):
+        cut = slice(64 * q, 64 * q + CHI)
+        rows[240 + 16 * q : 256 + 16 * q] = jnp.concatenate(
+            [first[48:64, cut], second[48:64, cut], pad[0:16]], axis=1
+        )
     rows[288:304] = jnp.zeros((16, 128), jnp.float32)
     for k in range(PEERS):
         ready[k] = rows[ROWS * k : ROWS * k + 16].astype(BF16)
@@ -301,8 +311,8 @@
     await_sent(0, pieces.at[0 : counts[0] // 2])
     await_sent(5, t2s.at[0])
     await_sent(1, t1x)
-    await_sent(2, from_z.at[0:3])
-    await_sent(3, extra_z.at[0:3])
+    await_sent(2, from_z.at[0, 0:3])
+    await_sent(3, from_z.at[1, 0:3])
     await_sent(4, arrived.at[0 : PEERS - 1])
 
 
@@ -324,16 +334,15 @@
             pltpu.VMEM((2, CHI * CHI, 128), jnp.float32),
             pltpu.VMEM((CHI * CHI, LANES), BF16),
             pltpu.VMEM((72 * CHI, 3 * LANES), jnp.float32),
-            pltpu.VMEM((GROUPS, 3 * NB * CHI, LANES), BF16),
-            pltpu.VMEM((GROUPS, 3 * NB * CHI, LANES), BF16),
-            pltpu.VMEM((GROUPS, 144, LANES), jnp.float32),
+            pltpu.VMEM((GROUPS, STEP, LANES), BF16),
+            pltpu.VMEM((GROUPS, STEP, LANES), BF16),
+            pltpu.VMEM((GROUPS, CHI, LANES), jnp.float32),
+            pltpu.VMEM((GROUPS, CHI, LANES), jnp.float32),
             pltpu.VMEM((3 * 72, TILE), BF16),
             pltpu.VMEM((PEERS, 2, 48, LANES), BF16),
             pltpu.VMEM((3 * LANES, GROUPS * LANES), BF16),
-            pltpu.VMEM((GROUPS, 96, LANES), BF16),
-            pltpu.VMEM((4, CHI, 128), BF16),
-            pltpu.VMEM((4, 96, LANES), BF16),
-            pltpu.VMEM((4, CHI, 128), BF16),
+            pltpu.VMEM((2, 4, 64, LANES), BF16),
+            pltpu.VMEM((2, 4, 64, LANES), BF16),
             pltpu.VMEM((304, 128), jnp.float32),
             pltpu.VMEM((PEERS, 16, 128), BF16),
             pltpu.VMEM((PEERS, 16, 128), BF16),
@@ -341,8 +350,7 @@
             dma((6,)),
             dma,
             dma((PEERS, 2)),
-            dma,
-            dma,
+            dma((2,)),
             dma,
         ],
         compiler_params=pltpu.CompilerParams(

time: 51.1 us -> 49.1 us (0.961)
  Pallas kernels: 49.9 us -> 47.8 us
    pallas_call x1, Pallas kernels: 49.9 us -> 47.8 us  [local(): pl.pallas_call(kernel, out_shape=OUT, in_specs=[pl.BlockSpec(memory_space...]
where the time goes in v7:
time: 49.1 us; the launch traced here: 48.5 us
  Pallas kernels  47.8 us (97%)
  local copies, waits for them, and re-layouts  0.64 us (1%)
    pallas_call x1, Pallas kernels, local(): pl.pallas_call(kernel, out_shape=OUT, in_specs=[pl.BlockSpec(memory_space...  47.8 us

profile of v7, /device:TPU:8, one launch (start us, length us, event | category | flops | bytes accessed | tf_op | source)
XLA Modules:
  0.0 48.5 jit_solution(17153396283754484924)
XLA Ops:
  0.0 47.8 %shard_map.46 = bf16[9,2304]{1,0:T(8,128)(2,1)S(1)} custom-call(bf16[72,288]{1,0:T(8,128)(2,1)} %t1_hbm.1, bf16[9,2304]{1,0:T(8,128)(2,1)} %t2_hbm.1, bf16[48,2304]{1,0:T(8,128)(2,1)} %bitcast.2, bf16[48,2304]{1,0:T(8,128)(2,1)} %bitcast.3), custom_call_target="tpu_custom_call" | custom-call | tf_op jit(solution)/shard_map/pallas_call | solution.py:321
  47.8 0.6 %copy.6 = bf16[9,2304]{1,0:T(8,128)(2,1)} copy(bf16[9,2304]{1,0:T(8,128)(2,1)S(1)} %shard_map.46) | data formatting | bytes 82944

commit v8 on v7

--- a/solution.py
+++ b/solution.py
@@ -15,13 +15,17 @@
 OUT = pltpu.VMEM((9, 2304), jnp.bfloat16)
 PEERS = 32
 FAR = (3, 1, 2)
+NEXT = (3, 1)
 MESH = pl.DeviceIdType.MESH
 BF16 = jnp.bfloat16
 SLOTS = (0, 1, 3, 4)
 
 
+STARTS = ((0, 9, 0), (16, 9, 0), (32, 9, 0), (9, 7, 9), (27, 5, 9))
+
+
 def row_window(g):
-    return min(ROWS * g // 16 * 16, 16)
+    return ((0, 16), (16, 16), (32, 16), (0, 32), (16, 32))[g]
 
 
 def f32dot(a, b):
@@ -37,7 +41,7 @@
 def kernel(
     t1_hbm, t2_hbm, pl_hbm, pr_hbm, out_ref,
     t1_ref, t2_ref, pl_ref, pr_ref, t1x, spread, t2s, plt, prt, wf, yb0, yb1, acc_half, acc_whole, t1s, pieces, t2p,
-    part, from_z, rows, ready, arrived,
+    part, from_z, turn, summed, ready, arrived,
     loaded, sent, t1_got, piece_got, z_got, row_got,
 ):
     i = lax.axis_index("row")
@@ -46,10 +50,15 @@
     core, zl = lax.rem(j, 2), j // 2
     other = 1 - core
     twin = 2 * zl + other
-    zpeers = [(lax.rem(zl + k, 4), 2 * lax.rem(zl + k, 4) + core) for k in range(1, 4)]
-
     def row_of(dz, dy, dx):
         return (lax.rem(y + dy, 4) * 2 + lax.rem(zh + dz, 2)) * 4 + lax.rem(x + dx, 4)
+
+    ring = []
+    for dz in range(2):
+        for k in range(4):
+            z = lax.rem(zl + k, 4)
+            where = {"row": row_of(dz, 0, 0), "col": 2 * z + core}
+            ring.append((z, lax.rem(zh + dz, 2), where))
 
     loads = []
     for k, (src, dst) in enumerate(
@@ -58,11 +67,12 @@
         loads.append(pltpu.make_async_copy(src, dst, loaded.at[k]))
         loads[-1].start()
     barrier = pltpu.get_barrier_semaphore()
-    near = [row_of(0, 0, k) for k in FAR] + [row_of(0, k, 0) for k in FAR] + [row_of(1, 0, 0)]
+    near = [row_of(0, 0, k) for k in FAR] + [row_of(0, k, 0) for k in FAR]
     for peer in near:
         pl.semaphore_signal(barrier, inc=1, device_id={"row": peer}, device_id_type=MESH)
-    for col in [twin] + [col for _, col in zpeers]:
-        pl.semaphore_signal(barrier, inc=1, device_id={"col": col}, device_id_type=MESH)
+    pl.semaphore_signal(barrier, inc=1, device_id={"col": twin}, device_id_type=MESH)
+    for _, _, where in ring[1:]:
+        pl.semaphore_signal(barrier, inc=1, device_id=where, device_id_type=MESH)
 
     spread[...] = jnp.zeros_like(spread)
     loads[0].wait()
@@ -70,14 +80,19 @@
     for c in range(2):
         for z in range(4):
             at = 6 * CHI * (2 * z + c)
-            spread[c, ROWS * z : ROWS * z + ROWS, 0 : 5 * CHI] = t2[:, at : at + 5 * CHI]
             slot = CHI * SLOTS[z]
-            spread[c, 4 * ROWS : 5 * ROWS, slot : slot + CHI] = t2[:, at + 5 * CHI : at + 6 * CHI]
+            for g, left, lanes, width in ((z, at, 0, 5 * CHI), (4, at + 5 * CHI, slot, CHI)):
+                row, run, skip = STARTS[g]
+                value = t2[:, left : left + width]
+                spread[c, row : row + run, lanes : lanes + width] = value[0:run]
+                if run < ROWS:
+                    to = row + run + skip
+                    spread[c, to : to + ROWS - run, lanes : lanes + width] = value[run:ROWS]
     t2s[...] = spread[...].astype(BF16)
     pieces[i, core] = t2s[core]
     loads[1].wait()
 
-    pl.semaphore_wait(barrier, 7 + 1 + 3)
+    pl.semaphore_wait(barrier, 6 + 1 + 7)
 
     counts = [0] * 6
 
@@ -148,9 +163,9 @@
 
     send(5, t2s.at[other], pieces.at[i, core], piece_got.at[i, core], {"col": twin})
     send(1, t1_ref, t1x, t1_got, {"col": twin})
-    pass_on(0, 0, 0, 0, to_z=(1,), to_a=FAR, to_b=FAR)
+    pass_on(0, 0, 0, 0, to_z=(1,), to_a=FAR, to_b=NEXT)
     await_piece(1, 0, 0, 0)
-    pass_on(1, 0, 0, 0, to_z=(1,), to_a=FAR, to_b=FAR)
+    pass_on(1, 0, 0, 0, to_z=(1,), to_a=FAR, to_b=NEXT)
 
     place_right = one_hot((CHI, LANES), lambda r, c: (r == c % CHI) & (c < 5 * CHI))
     loads[2].wait()
@@ -160,6 +175,8 @@
         for h in range(2):
             plt[h, pl.ds(k, CHI, stride=CHI), :] = z[:, 128 * h : 128 * h + 128]
     acc_half[...] = jnp.zeros_like(acc_half)
+    turn[...] = jnp.zeros_like(turn)
+    summed[...] = jnp.zeros_like(summed)
     acc_whole[...] = jnp.zeros_like(acc_whole)
     await_copy(t1x, t1_got)
     mine, theirs = t1_ref[...].astype(jnp.float32), t1x[...].astype(jnp.float32)
@@ -178,35 +195,48 @@
         for cr in range(2):
             for a in FAR:
                 await_piece(cr, dz, a, 0)
-                pass_on(cr, dz, a, 0, to_b=FAR)
+                pass_on(cr, dz, a, 0, to_b=FAR if dz else NEXT)
+
+    def relay_near():
+        for cr in range(2):
+            for a in (0, *FAR):
+                await_piece(cr, 0, a, 1)
+                pass_on(cr, 0, a, 1, to_b=(3,))
 
     def collect(dz):
         for cr in range(2):
             for a in (0, *FAR):
                 for b in FAR:
-                    await_piece(cr, dz, a, b)
+                    if dz == 1 or b != 1:
+                        await_piece(cr, dz, a, b)
 
     def pack(g):
-        w = row_window(g)
+        w, height = row_window(g)
+        row, run, skip = STARTS[g]
         for v in range(3):
-            pick = one_hot(
-                (CHI, 6 * 32),
-                lambda r, c: c == (r + 3 * v) // ROWS * 32 + ROWS * g - w + (r + 3 * v) % ROWS,
-            )
+
+            def hit(r, c):
+                q = (r + 3 * v) % ROWS
+                return c == (r + 3 * v) // ROWS * height + row - w + q + jnp.where(q < run, 0, skip)
+
+            pick = one_hot((CHI, 6 * height), hit)
             for m in range(v, 12, 3):
                 first = CHI * (m % 6) // ROWS
-                source = pieces[first : first + 6, m // 6, w : w + 32, :].reshape(192, LANES)
+                source = pieces[first : first + 6, m // 6, w : w + height, :]
+                source = source.reshape(6 * height, LANES)
                 to = LANES * (m // 4) + CHI * (m % 4)
                 t2p[to : to + CHI, LANES * g : LANES * g + LANES] = f32dot(pick, source).astype(BF16)
 
     weigh_some(2)
     relay(0)
-    weigh_some(2)
+    weigh_some(1)
     for cr in range(2):
         await_piece(cr, 1, 0, 0)
         pass_on(cr, 1, 0, 0, to_a=FAR, to_b=FAR)
+    relay_near()
+    weigh_some(1)
+    relay(1)
     weigh_some(2)
-    relay(1)
     loads[3].wait()
     prt[...] = lax.dot_general(
         pr_ref[...], place_right, (((0,), (0,)), ((), ())), preferred_element_type=jnp.float32
@@ -245,20 +275,21 @@
                 project(*before)
             yb[g] = f32dot(w, t2p[:, g * LANES : (g + 1) * LANES]).astype(BF16)
 
-    gap = jnp.zeros((16, 16), jnp.float32)
-    wide_gap = jnp.zeros((16, 64), jnp.float32)
-
     def send_part(u, total):
         for z in range(4):
-            part[u, z, 0:48, :] = total[z].astype(BF16)
+            for e in range(5):
+                turn[z, CHI * e : CHI * e + CHI, 0:CHI] = total[z][:, CHI * e : CHI * e + CHI]
             at = CHI * SLOTS[z]
-            sixth = total[4][:, at : at + CHI]
-            parts = []
-            for q in range(3):
-                parts += [sixth[16 * q : 16 * q + 16], gap]
-            part[u, z, 48:64, :] = jnp.concatenate(parts + [wide_gap], axis=1).astype(BF16)
-        for z, col in zpeers:
-            send(2 + u, part.at[u, z], from_z.at[u, zl], z_got.at[u], {"col": col})
+            turn[z, 5 * CHI : 6 * CHI, 0:CHI] = total[4][:, at : at + CHI]
+        for z in range(4):
+            for h in range(2):
+                low = [turn[z, 72 * q + 36 * h : 72 * q + 36 * h + 40, :] for q in range(4)]
+                part[u, z, h] = jnp.concatenate(
+                    [low[q] + pltpu.roll(low[2 + q], 64, 1) for q in range(2)], axis=0
+                ).astype(BF16)
+        from_z[u, 4 * zh + zl] = part[u, zl, zh]
+        for z, h, where in ring[1:]:
+            send(2 + u, part.at[u, z, h], from_z.at[u, 4 * zh + zl], z_got.at[u], where)
 
     jobs = [(base[0] + SLOTS_HERE * k, acc_half) for k in range(2)]
     jobs += [(base[1] + SLOTS_HERE * k, acc_whole) for k in range(4)]
@@ -272,48 +303,54 @@
     project(*before)
     send_part(1, acc_whole)
 
-    summed = []
     for u in range(2):
-        await_copy(from_z.at[u, 0:3], z_got.at[u])
-        value = part[u, zl].astype(jnp.float32)
-        for z, _ in zpeers:
-            value += from_z[u, z].astype(jnp.float32)
-        summed.append(value)
-    first = jnp.where(p == 0, summed[1], summed[0])
-    second = jnp.where(p == 0, summed[0], summed[1])
-    pad = jnp.zeros((CHI, 32), jnp.float32)
-    for e in range(5):
-        cut = slice(CHI * e, CHI * e + CHI)
-        rows[CHI * e : CHI * e + CHI] = jnp.concatenate(
-            [first[0:48, cut], second[0:48, cut], pad], axis=1
-        )
-    for q in range(3):
-        cut = slice(64 * q, 64 * q + CHI)
-        rows[240 + 16 * q : 256 + 16 * q] = jnp.concatenate(
-            [first[48:64, cut], second[48:64, cut], pad[0:16]], axis=1
-        )
-    rows[288:304] = jnp.zeros((16, 128), jnp.float32)
-    for k in range(PEERS):
-        ready[k] = rows[ROWS * k : ROWS * k + 16].astype(BF16)
-
-    for k in range(1, PEERS):
-        target = lax.rem(i + k, PEERS)
-        send(4, ready.at[target], arrived.at[i], row_got, {"row": target})
-    arrived[i] = ready[i]
-    await_copy(arrived.at[0 : PEERS - 1], row_got)
+        await_copy(from_z.at[u, 0:7], z_got.at[u])
+    for h in range(2):
+        half, whole = [
+            sum(from_z[u, 4 * h + z].astype(jnp.float32) for z in range(4)) for u in range(2)
+        ]
+        summed[2 * h, 0:80, :] = jnp.where(p == 0, whole, half)
+        summed[2 * h + 1, 0:80, :] = jnp.where(p == 0, half, whole)
+    wide = lax.broadcasted_iota(jnp.int32, (16, 128), 1)
+    for yt in range(4):
+        for xt in range(4):
+            at = 40 * (yt % 2) + ROWS * xt
+            sides = []
+            for h in range(2):
+                first, second = [summed[2 * h + f, at : at + 16, :] for f in range(2)]
+                if yt < 2:
+                    second = pltpu.roll(second, 64, 1)
+                else:
+                    first = pltpu.roll(first, 64, 1)
+                sides.append(jnp.where(wide < 64, first, second))
+            ready[4 * yt + xt] = jnp.concatenate(sides, axis=1).astype(BF16)
+
+    spot = 4 * y + x
+    for dy in range(4):
+        for dx in range(4):
+            if dy or dx:
+                target = 4 * lax.rem(y + dy, 4) + lax.rem(x + dx, 4)
+                where = {"row": row_of(0, dy, dx)}
+                send(4, ready.at[target], arrived.at[spot], row_got, where)
+    arrived[spot] = ready[spot]
+    await_copy(arrived.at[0:15], row_got)
     blocks = []
     for t in range(16):
-        even, odd = arrived[2 * t].astype(jnp.float32), arrived[2 * t + 1].astype(jnp.float32)
-        blocks += [even[:, 0:48], even[:, 48:96] + odd[:, 0:48], odd[:, 48:96]]
+        source, h = 4 * (t // 4) + 2 * (t % 2), t // 2 % 2
+        even, odd = [arrived[source + k].astype(jnp.float32) for k in range(2)]
+        one, two = 128 * h, 128 * h + 64
+        blocks.append(even[:, one : one + CHI])
+        blocks.append(even[:, two : two + CHI] + odd[:, one : one + CHI])
+        blocks.append(odd[:, two : two + CHI])
     out_ref[...] = jnp.concatenate(blocks, axis=1)[0:ROWS].astype(BF16)
 
-    assert counts == [2 * (counts[0] // 2), 1, 3, 3, PEERS - 1, 1], counts
+    assert counts == [2 * (counts[0] // 2), 1, 7, 7, 15, 1], counts
     await_sent(0, pieces.at[0 : counts[0] // 2])
     await_sent(5, t2s.at[0])
     await_sent(1, t1x)
-    await_sent(2, from_z.at[0, 0:3])
-    await_sent(3, from_z.at[1, 0:3])
-    await_sent(4, arrived.at[0 : PEERS - 1])
+    await_sent(2, from_z.at[0, 0:7])
+    await_sent(3, from_z.at[1, 0:7])
+    await_sent(4, arrived.at[0:15])
 
 
 def local(top_tensor, bottom_tensor, left_proj, right_proj):
@@ -341,11 +378,12 @@
             pltpu.VMEM((3 * 72, TILE), BF16),
             pltpu.VMEM((PEERS, 2, 48, LANES), BF16),
             pltpu.VMEM((3 * LANES, GROUPS * LANES), BF16),
-            pltpu.VMEM((2, 4, 64, LANES), BF16),
-            pltpu.VMEM((2, 4, 64, LANES), BF16),
-            pltpu.VMEM((304, 128), jnp.float32),
-            pltpu.VMEM((PEERS, 16, 128), BF16),
-            pltpu.VMEM((PEERS, 16, 128), BF16),
+            pltpu.VMEM((2, 4, 2, 80, 128), BF16),
+            pltpu.VMEM((2, 8, 80, 128), BF16),
+            pltpu.VMEM((4, 296, 128), jnp.float32),
+            pltpu.VMEM((4, 88, 128), jnp.float32),
+            pltpu.VMEM((16, 16, LANES), BF16),
+            pltpu.VMEM((16, 16, LANES), BF16),
             dma((4,)),
             dma((6,)),
             dma,

time: 49.1 us -> 48.2 us (0.982)
  Pallas kernels: 47.8 us -> 46.8 us
    pallas_call x1, Pallas kernels: 47.8 us -> 46.8 us  [local(): pl.pallas_call(kernel, out_shape=OUT, in_specs=[pl.BlockSpec(memory_space...]
where the time goes in v8:
time: 48.2 us; the launch traced here: 47.4 us
  Pallas kernels  46.8 us (97%)
  local copies, waits for them, and re-layouts  0.64 us (1%)
    pallas_call x1, Pallas kernels, local(): pl.pallas_call(kernel, out_shape=OUT, in_specs=[pl.BlockSpec(memory_space...  46.8 us

profile of v8, /device:TPU:8, one launch (start us, length us, event | category | flops | bytes accessed | tf_op | source)
XLA Modules:
  0.0 47.4 jit_solution(17416674399085653213)
XLA Ops:
  0.0 46.8 %shard_map.46 = bf16[9,2304]{1,0:T(8,128)(2,1)S(1)} custom-call(bf16[72,288]{1,0:T(8,128)(2,1)} %t1_hbm.1, bf16[9,2304]{1,0:T(8,128)(2,1)} %t2_hbm.1, bf16[48,2304]{1,0:T(8,128)(2,1)} %bitcast.2, bf16[48,2304]{1,0:T(8,128)(2,1)} %bitcast.3), custom_call_target="tpu_custom_call" | custom-call | tf_op jit(solution)/shard_map/pallas_call | solution.py:358
  46.8 0.6 %copy.6 = bf16[9,2304]{1,0:T(8,128)(2,1)} copy(bf16[9,2304]{1,0:T(8,128)(2,1)S(1)} %shard_map.46) | data formatting | bytes 82944

commit v9 on v8

--- a/solution.py
+++ b/solution.py
@@ -118,18 +118,25 @@
     def block(cr):
         return core if cr == 0 else other
 
+    def place_got(cr, dz, a, b):
+        if b == 0:
+            return 16 * cr + 8 * dz + a
+        if b == 1 and dz == 0:
+            return 16 * cr + 4 + a
+        return 16 * cr + 12 + dz
+
     def pass_on(cr, dz, a, b, to_z=(), to_a=(), to_b=()):
         source, c = place(cr, dz, a, b), block(cr)
         own = cr == 0 and dz == 0 and a == 0 and b == 0
         src = t2s.at[core] if own else pieces.at[source, c]
-        targets = [place(cr, 1, 0, 0) for _ in to_z]
-        targets += [place(cr, 0, t, 0) for t in to_a] + [place(cr, 0, 0, t) for t in to_b]
-        for target in targets:
-            send(0, src, pieces.at[source, c], piece_got.at[source, c], {"row": target})
+        targets = [(place(cr, 1, 0, 0), place_got(cr, 1, 0, 0)) for _ in to_z]
+        targets += [(place(cr, 0, t, 0), place_got(cr, dz, (a - t) % 4, b)) for t in to_a]
+        targets += [(place(cr, 0, 0, t), place_got(cr, dz, a, (b - t) % 4)) for t in to_b]
+        for target, got in targets:
+            send(0, src, pieces.at[source, c], piece_got.at[got], {"row": target})
 
     def await_piece(cr, dz, a, b):
-        source, c = place(cr, dz, a, b), block(cr)
-        await_copy(pieces.at[source, c], piece_got.at[source, c])
+        await_copy(pieces.at[place(cr, dz, a, b), block(cr)], piece_got.at[place_got(cr, dz, a, b)])
 
     lane = lax.broadcasted_iota(jnp.int32, (CHI, LANES), 1)
     zero = jnp.zeros((CHI, LANES), BF16)
@@ -161,7 +168,7 @@
         lax.fori_loop(done[0], done[0] + count, weigh, 0)
         done[0] += count
 
-    send(5, t2s.at[other], pieces.at[i, core], piece_got.at[i, core], {"col": twin})
+    send(5, t2s.at[other], pieces.at[i, core], piece_got.at[16], {"col": twin})
     send(1, t1_ref, t1x, t1_got, {"col": twin})
     pass_on(0, 0, 0, 0, to_z=(1,), to_a=FAR, to_b=NEXT)
     await_piece(1, 0, 0, 0)
@@ -205,10 +212,7 @@
 
     def collect(dz):
         for cr in range(2):
-            for a in (0, *FAR):
-                for b in FAR:
-                    if dz == 1 or b != 1:
-                        await_piece(cr, dz, a, b)
+            await_copy(pieces.at[0 : 6 if dz else 4], piece_got.at[16 * cr + 12 + dz])
 
     def pack(g):
         w, height = row_window(g)
@@ -387,7 +391,7 @@
             dma((4,)),
             dma((6,)),
             dma,
-            dma((PEERS, 2)),
+            dma((32,)),
             dma((2,)),
             dma,
         ],

time: 48.2 us -> 47.9 us (level)
  no operation moved by 1% of the time
where the time goes in v9:
time: 47.9 us; the launch traced here: 47.2 us
  Pallas kernels  46.6 us (97%)
  local copies, waits for them, and re-layouts  0.64 us (1%)
    pallas_call x1, Pallas kernels, local(): pl.pallas_call(kernel, out_shape=OUT, in_specs=[pl.BlockSpec(memory_space...  46.6 us

profile of v9, /device:TPU:8, one launch (start us, length us, event | category | flops | bytes accessed | tf_op | source)
XLA Modules:
  0.0 47.2 jit_solution(17588230020037960881)
XLA Ops:
  0.0 46.6 %shard_map.46 = bf16[9,2304]{1,0:T(8,128)(2,1)S(1)} custom-call(bf16[72,288]{1,0:T(8,128)(2,1)} %t1_hbm.1, bf16[9,2304]{1,0:T(8,128)(2,1)} %t2_hbm.1, bf16[48,2304]{1,0:T(8,128)(2,1)} %bitcast.2, bf16[48,2304]{1,0:T(8,128)(2,1)} %bitcast.3), custom_call_target="tpu_custom_call" | custom-call | tf_op jit(solution)/shard_map/pallas_call | solution.py:362
  46.6 0.6 %copy.6 = bf16[9,2304]{1,0:T(8,128)(2,1)} copy(bf16[9,2304]{1,0:T(8,128)(2,1)S(1)} %shard_map.46) | data formatting | bytes 82944

commit v10 on v9

--- a/solution.py
+++ b/solution.py
@@ -90,6 +90,13 @@
                     spread[c, to : to + ROWS - run, lanes : lanes + width] = value[run:ROWS]
     t2s[...] = spread[...].astype(BF16)
     pieces[i, core] = t2s[core]
+    place_right = one_hot((CHI, LANES), lambda r, c: (r == c % CHI) & (c < 5 * CHI))
+    loads[2].wait()
+    left_proj = pl_ref[...].astype(jnp.float32)
+    for k in range(CHI):
+        z = f32dot(left_proj[:, CHI * k : CHI * k + CHI].astype(BF16), place_right)
+        for h in range(2):
+            plt[h, pl.ds(k, CHI, stride=CHI), :] = z[:, 128 * h : 128 * h + 128]
     loads[1].wait()
 
     pl.semaphore_wait(barrier, 6 + 1 + 7)
@@ -174,13 +181,6 @@
     await_piece(1, 0, 0, 0)
     pass_on(1, 0, 0, 0, to_z=(1,), to_a=FAR, to_b=NEXT)
 
-    place_right = one_hot((CHI, LANES), lambda r, c: (r == c % CHI) & (c < 5 * CHI))
-    loads[2].wait()
-    left_proj = pl_ref[...].astype(jnp.float32)
-    for k in range(CHI):
-        z = f32dot(left_proj[:, CHI * k : CHI * k + CHI].astype(BF16), place_right)
-        for h in range(2):
-            plt[h, pl.ds(k, CHI, stride=CHI), :] = z[:, 128 * h : 128 * h + 128]
     acc_half[...] = jnp.zeros_like(acc_half)
     turn[...] = jnp.zeros_like(turn)
     summed[...] = jnp.zeros_like(summed)
@@ -231,14 +231,13 @@
                 to = LANES * (m // 4) + CHI * (m % 4)
                 t2p[to : to + CHI, LANES * g : LANES * g + LANES] = f32dot(pick, source).astype(BF16)
 
-    weigh_some(2)
+    weigh_some(1)
     relay(0)
-    weigh_some(1)
     for cr in range(2):
         await_piece(cr, 1, 0, 0)
         pass_on(cr, 1, 0, 0, to_a=FAR, to_b=FAR)
     relay_near()
-    weigh_some(1)
+    weigh_some(3)
     relay(1)
     weigh_some(2)
     loads[3].wait()

time: 47.9 us -> 47.7 us (level); the launches traced: 47.2 us -> 47.6 us
  no operation moved by 1% of the time
where the time goes in v10:
time: 47.7 us; the launch traced here: 47.6 us
  Pallas kernels  46.9 us (98%)
  local copies, waits for them, and re-layouts  0.64 us (1%)
    pallas_call x1, Pallas kernels, local(): pl.pallas_call(kernel, out_shape=OUT, in_specs=[pl.BlockSpec(memory_space...  46.9 us

profile of v10, /device:TPU:8, one launch (start us, length us, event | category | flops | bytes accessed | tf_op | source)
XLA Modules:
  0.0 47.6 jit_solution(4793367284363784505)
XLA Ops:
  0.0 46.9 %shard_map.46 = bf16[9,2304]{1,0:T(8,128)(2,1)S(1)} custom-call(bf16[72,288]{1,0:T(8,128)(2,1)} %t1_hbm.1, bf16[9,2304]{1,0:T(8,128)(2,1)} %t2_hbm.1, bf16[48,2304]{1,0:T(8,128)(2,1)} %bitcast.2, bf16[48,2304]{1,0:T(8,128)(2,1)} %bitcast.3), custom_call_target="tpu_custom_call" | custom-call | tf_op jit(solution)/shard_map/pallas_call | solution.py:361
  46.9 0.6 %copy.6 = bf16[9,2304]{1,0:T(8,128)(2,1)} copy(bf16[9,2304]{1,0:T(8,128)(2,1)S(1)} %shard_map.46) | data formatting | bytes 82944

commit v11 on v10

--- a/solution.py
+++ b/solution.py
@@ -181,10 +181,6 @@
     await_piece(1, 0, 0, 0)
     pass_on(1, 0, 0, 0, to_z=(1,), to_a=FAR, to_b=NEXT)
 
-    acc_half[...] = jnp.zeros_like(acc_half)
-    turn[...] = jnp.zeros_like(turn)
-    summed[...] = jnp.zeros_like(summed)
-    acc_whole[...] = jnp.zeros_like(acc_whole)
     await_copy(t1x, t1_got)
     mine, theirs = t1_ref[...].astype(jnp.float32), t1x[...].astype(jnp.float32)
     lower = jnp.where(core == 0, mine, theirs)
@@ -193,11 +189,6 @@
     t1s[...] = jnp.concatenate(
         [both[:, TILE * t : TILE * t + TILE] for t in range(3)], axis=0
     ).astype(BF16)
-    for t in range(3):
-        t2p[LANES * t + TILE : LANES * t + LANES, :] = jnp.zeros(
-            (LANES - TILE, GROUPS * LANES), BF16
-        )
-
     def relay(dz):
         for cr in range(2):
             for a in FAR:
@@ -240,6 +231,14 @@
     weigh_some(3)
     relay(1)
     weigh_some(2)
+    acc_half[...] = jnp.zeros_like(acc_half)
+    turn[...] = jnp.zeros_like(turn)
+    summed[...] = jnp.zeros_like(summed)
+    acc_whole[...] = jnp.zeros_like(acc_whole)
+    for t in range(3):
+        t2p[LANES * t + TILE : LANES * t + LANES, :] = jnp.zeros(
+            (LANES - TILE, GROUPS * LANES), BF16
+        )
     loads[3].wait()
     prt[...] = lax.dot_general(
         pr_ref[...], place_right, (((0,), (0,)), ((), ())), preferred_element_type=jnp.float32

time: 47.7 us -> 47.7 us (level)
  no operation moved by 1% of the time
where the time goes in v11:
time: 47.7 us; the launch traced here: 47.6 us
  Pallas kernels  46.9 us (98%)
  local copies, waits for them, and re-layouts  0.64 us (1%)
    pallas_call x1, Pallas kernels, local(): pl.pallas_call(kernel, out_shape=OUT, in_specs=[pl.BlockSpec(memory_space...  46.9 us

profile of v11, /device:TPU:8, one launch (start us, length us, event | category | flops | bytes accessed | tf_op | source)
XLA Modules:
  0.0 47.6 jit_solution(700970877278916371)
XLA Ops:
  0.0 46.9 %shard_map.46 = bf16[9,2304]{1,0:T(8,128)(2,1)S(1)} custom-call(bf16[72,288]{1,0:T(8,128)(2,1)} %t1_hbm.1, bf16[9,2304]{1,0:T(8,128)(2,1)} %t2_hbm.1, bf16[48,2304]{1,0:T(8,128)(2,1)} %bitcast.2, bf16[48,2304]{1,0:T(8,128)(2,1)} %bitcast.3), custom_call_target="tpu_custom_call" | custom-call | tf_op jit(solution)/shard_map/pallas_call | solution.py:360
  46.9 0.6 %copy.6 = bf16[9,2304]{1,0:T(8,128)(2,1)} copy(bf16[9,2304]{1,0:T(8,128)(2,1)S(1)} %shard_map.46) | data formatting | bytes 82944
